TPU v7x, 16 devices: a whole 2x2x2 slice. The times are simulated.
16 devices in a mesh: data: 16 (over z, y, x, core).
Axes of the slice: x: 2, y: 2, z: 2, core: 2. Of those that a mesh axis runs over, the one named last changes fastest.
Arguments:
- q_in: bfloat16 [8192, 384], P('data')
- d_in: bfloat16 [2, 8192, 384], P(None, 'data')
- temperature: float32 [], replicated
- q_w1: bfloat16 [2, 384, 1536], replicated
- q_w2: bfloat16 [2, 1536, 384], replicated
- q_proj: bfloat16 [384, 384], replicated
- d_w1: bfloat16 [2, 384, 1536], replicated
- d_w2: bfloat16 [2, 1536, 384], replicated
- d_proj: bfloat16 [384, 384], replicated
Outputs:
- output 1: float32 [], replicated
- output 2: float32 [2, 384, 1536], replicated
- output 3: float32 [2, 1536, 384], replicated
- output 4: float32 [384, 384], replicated
- output 5: float32 [2, 384, 1536], replicated
- output 6: float32 [2, 1536, 384], replicated
- output 7: float32 [384, 384], replicated
All inputs are finite; a program needn't handle non-finite values.
Results may differ from a plain program's by a relative error of at most 0.00545337.
Values are sent between devices in bfloat16 or wider.
A program may use at most 1 GiB of HBM per device.

v0:
```python
import jax
import jax.numpy as jnp
from jax import lax
from jax.sharding import PartitionSpec as P

SUB_COUNT = 4
ROWS_CONTRACT = (((0,), (0,)), ((), ()))
LAST_CONTRACT = (((1,), (1,)), ((), ()))


def tower_forward(row_block, w_one, w_two, w_proj):
    hidden = row_block
    saved = []
    for layer in range(2):
        pre_act = jnp.dot(hidden, w_one[layer], preferred_element_type=jnp.float32)
        act_bf = jax.nn.gelu(pre_act).astype(jnp.bfloat16)
        saved.append((hidden, pre_act, act_bf))
        hidden = (hidden.astype(jnp.float32) + jnp.dot(act_bf, w_two[layer], preferred_element_type=jnp.float32)).astype(jnp.bfloat16)
    out_reps = jnp.dot(hidden, w_proj, preferred_element_type=jnp.float32).astype(jnp.bfloat16)
    return out_reps, hidden, saved


def tower_backward(upstream, w_one, w_two, w_proj, hidden, saved):
    g_proj = lax.dot_general(hidden, upstream, ROWS_CONTRACT, preferred_element_type=jnp.float32)
    resid_grad = lax.dot_general(upstream, w_proj, LAST_CONTRACT, preferred_element_type=jnp.float32)
    grads_one = [None, None]
    grads_two = [None, None]
    for layer in (1, 0):
        h_in, pre_act, act_bf = saved[layer]
        resid_bf = resid_grad.astype(jnp.bfloat16)
        grads_two[layer] = lax.dot_general(act_bf, resid_bf, ROWS_CONTRACT, preferred_element_type=jnp.float32)
        act_grad = lax.dot_general(resid_bf, w_two[layer], LAST_CONTRACT, preferred_element_type=jnp.float32)
        gelu_back = jax.vjp(jax.nn.gelu, pre_act)[1]
        pre_grad = gelu_back(act_grad)[0].astype(jnp.bfloat16)
        grads_one[layer] = lax.dot_general(h_in, pre_grad, ROWS_CONTRACT, preferred_element_type=jnp.float32)
        if layer == 1:
            resid_grad = resid_grad + lax.dot_general(pre_grad, w_one[layer], LAST_CONTRACT, preferred_element_type=jnp.float32)
    return jnp.stack(grads_one), jnp.stack(grads_two), g_proj


def tower_grads(row_subs, up_subs, w_one, w_two, w_proj):
    def body(running, block_in):
        row_block, upstream = block_in
        hidden, saved = tower_forward(row_block, w_one, w_two, w_proj)[1:]
        new_grads = tower_backward(upstream, w_one, w_two, w_proj, hidden, saved)
        return tuple(old_sum + new_part for old_sum, new_part in zip(running, new_grads)), None

    zeros_init = (jnp.zeros(w_one.shape, jnp.float32), jnp.zeros(w_two.shape, jnp.float32), jnp.zeros(w_proj.shape, jnp.float32))
    return lax.scan(body, zeros_init, (row_subs, up_subs))[0]


def local_step(q_loc, d_loc, value_a11, q_w1, q_w2, q_proj, d_w1, d_w2, d_proj):
    rows_loc, width_in = q_loc.shape
    q_sub = q_loc.reshape(SUB_COUNT, rows_loc // SUB_COUNT, width_in)
    d_sub = d_loc.reshape(SUB_COUNT, 2 * rows_loc // SUB_COUNT, width_in)
    q_reps = lax.map(lambda row_block: tower_forward(row_block, q_w1, q_w2, q_proj)[0], q_sub).reshape(rows_loc, -1)
    d_reps = lax.map(lambda row_block: tower_forward(row_block, d_w1, d_w2, d_proj)[0], d_sub).reshape(2, rows_loc, -1)
    all_docs = lax.all_gather(d_reps, 'data', axis=1, tiled=True)
    global_batch = all_docs.shape[1]
    rep_width = all_docs.shape[2]
    doc_flat = all_docs.reshape(2 * global_batch, rep_width)
    logits = lax.dot_general(q_reps, doc_flat, LAST_CONTRACT, preferred_element_type=jnp.float32) / value_a11
    row_start = lax.axis_index('data') * rows_loc
    target = jnp.arange(2 * global_batch)[None, :] == (row_start + jnp.arange(rows_loc))[:, None]
    log_norm = jax.nn.logsumexp(logits, axis=1)
    pos_logit = jnp.sum(jnp.where(target, logits, 0.0), axis=1)
    loss = lax.psum(jnp.sum(log_norm - pos_logit), 'data') / global_batch
    soft_prob = jnp.exp(logits - log_norm[:, None])
    grad_logit = ((soft_prob - target.astype(jnp.float32)) / (global_batch * value_a11)).astype(jnp.bfloat16)
    q_up = jnp.dot(grad_logit, doc_flat, preferred_element_type=jnp.float32).astype(jnp.bfloat16)
    doc_part = lax.dot_general(grad_logit, q_reps, ROWS_CONTRACT, preferred_element_type=jnp.float32)
    doc_up = lax.psum_scatter(doc_part.reshape(2, global_batch, rep_width), 'data', scatter_dimension=1, tiled=True).astype(jnp.bfloat16)
    q_grads = tower_grads(q_sub, q_up.reshape(SUB_COUNT, -1, rep_width), q_w1, q_w2, q_proj)
    d_grads = tower_grads(d_sub, doc_up.reshape(SUB_COUNT, -1, rep_width), d_w1, d_w2, d_proj)
    q_one, q_two, q_pgrad = lax.psum(q_grads, 'data')
    d_one, d_two, d_pgrad = lax.psum(d_grads, 'data')
    return (loss, q_one, q_two, q_pgrad, d_one, d_two, d_pgrad)


def solution(mesh):
    specs_in = (P('data', None), P(None, 'data', None), P(), P(), P(), P(), P(), P(), P())
    specs_out = (P(), P(), P(), P(), P(), P(), P())
    return jax.shard_map(local_step, mesh=mesh, in_specs=specs_in, out_specs=specs_out, check_vma=False)
```

profile of v0, /device:TPU:0, one launch (start us, length us, event | category | flops | bytes accessed | tf_op | source)
XLA Modules:
  0.0 696.6 jit_solution(13590523202766310770)
XLA Ops:
  7.2 32.4 %while.57 = (s32[]{:T(128)}, bf16[4,256,384]{2,1,0:T(8,128)(2,1)}, bf16[4,256,384]{2,1,0:T(8,128)(2,1)}, bf16[2,384,1536]{2,1,0:T(8,128)(2,1)}, bf16[2,1536,384]...) while((s32[]{:T(128)}, bf16[4,256,384]{2,1,0:T(8,128)(2,1)}, bf16[4,256,384]{2,1,0:T(8,128)(2,1)}, ...), condition=%wide.region_3.4_spmd, body=%wide.region_2.3_spmd.sunk | while | flops 1291223040 | bytes 18384016 | solution.py:57
  7.2 3.6 fusion.424
  12.6 2.8 fusion.426
  15.4 3.6 fusion.424
  20.7 2.8 fusion.426
  23.4 3.6 fusion.424
  28.8 2.8 fusion.426
  31.5 3.6 fusion.424
  36.9 2.8 fusion.426
  40.5 23.6 %while.56 = (s32[]{:T(128)}, bf16[4,128,384]{2,1,0:T(8,128)(2,1)S(1)}, bf16[4,128,384]{2,1,0:T(8,128)(2,1)}, bf16[2,384,1536]{2,1,0:T(8,128)(2,1)}, bf16[2,1536,...) while((s32[]{:T(128)}, bf16[4,128,384]{2,1,0:T(8,128)(2,1)S(1)}, ...), condition=%wide.region_1.2_spmd, body=%wide.region_0.1_spmd.sunk | while | flops 645611520 | bytes 15828085 | solution.py:56
  40.5 2.4 fusion.413
  46.5 2.4 fusion.413
  52.4 2.4 fusion.413
  58.3 2.4 fusion.413
  64.2 40.7 %all-gather.2.cloned.1.call-done = bf16[2,8192,384]{2,1,0:T(8,128)(2,1)} async-done(((bf16[2,512,384]{2,1,0:T(8,128)(2,1)}), bf16[2,8192,384]{2,1,0:T(8,128)(2,1)}) %all-gather.2.cloned.1.call-update) | async-done | bytes 12582928 | tf_op jit(solution)/shard_map/all_gather | solution.py:58
  104.9 23.9 %fusion.304 = (f32[512]{0:T(512)S(1)}, f32[512,16384]{1,0:T(8,128)}) fusion(f32[]{:T(128)S(6)} %copy.62, bf16[512,384]{1,0:T(8,128)(2,1)S(1)} %bitcast.361, bf16[16384,384]{1,0:T(8,128)(2,1)} %bitcast.363), kind=kOutput, calls=%fused_computation.274 | convolution fusion | flops 6459227648 | bytes 46532612 | tf_op jit(solution)/shard_map/dot_general | solution.py:62
  128.8 17.3 %select_reduce_fusion = (f32[512]{0:T(512)S(1)}, f32[512]{0:T(512)S(1)}) fusion(f32[512,16384]{1,0:T(8,128)} %get-tuple-element.488, s32[512]{0:T(512)S(1)} %iota_add_fusion, f32[512]{0:T(512)S(1)} %is-finite_select_fusion), kind=kLoop, calls=%fused_computation.264 | loop fusion | flops 41942016 | bytes 33562624 | tf_op jit(solution)/shard_map/reduce_sum | solution.py:66
  146.7 2.3 copy-done
  149.0 11.0 %fusion.301 = bf16[16384,512]{0,1:T(8,128)(2,1)} fusion(f32[512,16384]{1,0:T(8,128)S(1)} %copy-done, f32[]{:T(128)S(6)} %mul.435, s32[512]{0:T(512)S(1)} %iota_add_fusion, f32[512]{0:T(512)S(1)} %get-tuple-element.486), kind=kLoop, calls=%fused_computation.260 | loop fusion | flops 50331648 | bytes 50335748 | tf_op jit(solution)/shard_map/convert_element_type | solution.py:69
  160.0 22.5 %copy.17 = bf16[16384,512]{1,0:T(8,128)(2,1)} copy(bf16[16384,512]{0,1:T(8,128)(2,1)} %fusion.301) | data formatting | bytes 33554432 | tf_op jit(solution)/shard_map/dot_general | solution.py:71
  182.5 17.0 %fusion.305 = f32[2,8192,384]{2,1,0:T(8,128)} fusion(bf16[2,8192,512]{2,1,0:T(8,128)(2,1)} %bitcast.353, bf16[512,384,1]{1,0,2:T(8,128)(2,1)S(1)} %bitcast.362), kind=kOutput, calls=%fused_computation.275 | convolution fusion | flops 6442450944 | bytes 42336256 | tf_op jit(solution)/shard_map/dot_general | solution.py:71
  199.8 20.8 %fusion.303 = bf16[512,384]{1,0:T(8,128)(2,1)} fusion(bf16[16384,384]{1,0:T(8,128)(2,1)} %bitcast.364, f32[512,16384]{1,0:T(8,128)} %get-tuple-element.488, f32[]{:T(128)S(6)} %mul.435, f32[512]{0:T(512)S(1)} %get-tuple-element.486, s32[512]{0:T(512)S(1)} %iota_add_fusion), kind=kOutput, calls=%fused_computation.269 | convolution fusion | flops 6492979200 | bytes 46534660 | tf_op jit(solution)/shard_map/dot_general | solution.py:70
  220.6 113.9 %while.58 = (s32[]{:T(128)}, f32[2,384,1536]{2,1,0:T(8,128)}, f32[2,1536,384]{2,1,0:T(8,128)}, f32[384,384]{1,0:T(8,128)}, bf16[4,128,384]{2,1,0:T(8,128)(2,1)},...) while((s32[]{:T(128)}, f32[2,384,1536]{2,1,0:T(8,128)}, ...), condition=%wide.region_10.11_spmd.clone, body=%wide.region_9.10_spmd.clone.sunk | while | flops 1759248384 | bytes 80511288 | solution.py:49
  230.4 3.8 convolution_bitcast_fusion.17
  234.2 5.0 maximum_add_fusion.8
  240.3 3.0 maximum_add_fusion.9
  243.3 2.1 convolution_add_fusion.9
  256.0 3.8 convolution_bitcast_fusion.17
  259.8 6.3 maximum_add_fusion.8
  267.3 5.4 maximum_add_fusion.9
  272.7 2.1 convolution_add_fusion.9
  285.4 3.8 convolution_bitcast_fusion.17
  289.2 6.3 maximum_add_fusion.8
  296.7 5.4 maximum_add_fusion.9
  302.1 2.1 convolution_add_fusion.9
  314.8 3.8 convolution_bitcast_fusion.17
  318.6 6.3 maximum_add_fusion.8
  326.1 5.4 maximum_add_fusion.9
  331.6 2.1 convolution_add_fusion.9
  334.4 2.9 reduce-scatter.2.cloned.1.call-done
  337.3 2.4 convert_element_type.205
  339.7 125.4 %while.59 = (s32[]{:T(128)}, f32[2,384,1536]{2,1,0:T(8,128)}, f32[2,1536,384]{2,1,0:T(8,128)}, f32[384,384]{1,0:T(8,128)}, bf16[4,256,384]{2,1,0:T(8,128)(2,1)},...) while((s32[]{:T(128)}, f32[2,384,1536]{2,1,0:T(8,128)}, ...), condition=%wide.region_16.17_spmd.clone, body=%wide.region_15.16_spmd.clone.sunk | while | flops 3511123968 | bytes 116294048 | solution.py:49
  349.6 4.9 convolution_bitcast_fusion.21
  354.5 5.0 maximum_add_fusion.10
  361.7 3.0 maximum_add_fusion.11
  364.7 3.0 convolution_add_fusion.10
  378.1 4.9 convolution_bitcast_fusion.21
  383.0 6.4 maximum_add_fusion.10
  391.5 5.4 maximum_add_fusion.11
  396.9 3.0 convolution_add_fusion.10
  410.3 4.9 convolution_bitcast_fusion.21
  415.2 6.4 maximum_add_fusion.10
  423.8 5.4 maximum_add_fusion.11
  429.2 3.0 convolution_add_fusion.10
  442.6 4.9 convolution_bitcast_fusion.21
  447.5 6.4 maximum_add_fusion.10
  456.0 5.4 maximum_add_fusion.11
  461.4 3.0 convolution_add_fusion.10
  465.2 32.8 %psum.49 = f32[]{:T(128)} all-reduce(f32[]{:T(128)} %get-tuple-element.485), channel_id=1, replica_groups=mesh['data'=16] {'data'}, use_global_device_ids=true, to_apply=%region_8.9 | all-reduce | flops 1 | bytes 8 | tf_op jit(solution)/shard_map/psum | solution.py:67
  498.6 174.1 %all-reduce.3.cloned.1.call-done = (f32[2,384,1536]{2,1,0:T(8,128)}, f32[2,1536,384]{2,1,0:T(8,128)}, f32[384,384]{1,0:T(8,128)}, f32[2,384,1536]{2,1,0:T(8,128)...) async-done(((f32[2,384,1536]{2,1,0:T(8,128)}, f32[2,1536,384]{2,1,0:T(8,128)}, f32[384,384]{1,0:T(8,128)}, f32[2,384,1536]{2,1,0:T(8,128)}, f32[2,1536,384]{2,1,0:T(8,128)}, ...) | async-done | bytes 20054032 | tf_op jit(solution)/shard_map/psum | solution.py:75
  672.7 5.2 copy.63
  677.9 2.4 copy.64
  682.0 2.4 copy.66
  685.5 2.2 copy.67
  (266 shorter events, 122.6 us)
Async XLA Ops:
  7.2 97.7 %all-gather.2.cloned.1.call-start = ((), (), s32[]{:S(2)}) async-start(), calls=%async_computation.1 | async-start | bytes 13369344 | tf_op jit(solution)/shard_map/all_gather | solution.py:58
  7.2 3.6 copy-start.4
  15.4 3.6 copy-start.4
  23.4 3.6 copy-start.4
  31.5 3.6 copy-start.4
  39.6 297.7 %reduce-scatter.2.cloned.1.call-start = ((), (), s32[]{:S(2)}) async-start(), calls=%async_computation.2 | async-start | bytes 26738688 | tf_op jit(solution)/shard_map/reduce_scatter | solution.py:72
  42.9 2.0 copy-start.20
  48.8 2.0 copy-start.20
  54.7 2.0 copy-start.20
  60.6 2.0 copy-start.20
  128.8 20.2 %copy-start = (f32[512,16384]{1,0:T(8,128)S(1)}, f32[512,16384]{1,0:T(8,128)}, u32[]{:S(2)}) copy-start(f32[512,16384]{1,0:T(8,128)} %get-tuple-element.488) | copy-start | bytes 100663296
  199.5 473.2 %all-reduce.3.cloned.1.call-start = ((), (), s32[]{:S(2)}) async-start(), calls=%async_computation.3 | async-start | bytes 40108032 | tf_op jit(solution)/shard_map/psum | solution.py:75
  224.0 3.3 copy-start.21
  225.8 2.3 copy-start.1
  234.2 5.0 copy-start.2
  240.3 3.0 copy-start.3
  240.3 3.0 copy-start.16
  249.6 3.4 copy-start.21
  251.4 2.3 copy-start.1
  259.8 6.3 copy-start.2
  267.3 5.4 copy-start.3
  267.3 5.4 copy-start.16
  279.0 3.3 copy-start.21
  280.8 2.3 copy-start.1
  289.2 6.3 copy-start.2
  296.7 5.4 copy-start.3
  296.7 5.4 copy-start.16
  308.4 3.3 copy-start.21
  310.2 2.3 copy-start.1
  318.6 6.3 copy-start.2
  326.1 5.4 copy-start.3
  326.1 5.4 copy-start.16
  334.4 5.3 copy-start.5
  340.0 1.8 copy-start.22
  341.7 1.8 copy-start.9
  344.1 3.1 copy-start.7
  354.5 5.0 copy-start.8
  361.7 3.0 copy-start.14
  364.7 3.8 copy-start.6
  368.4 1.8 copy-start.22
  370.2 1.8 copy-start.9
  372.6 3.1 copy-start.7
  383.0 6.4 copy-start.8
  391.5 5.4 copy-start.14
  396.9 3.8 copy-start.6
  400.7 1.8 copy-start.22
  402.4 1.8 copy-start.9
  404.9 3.1 copy-start.7
  415.2 6.4 copy-start.8
  423.8 5.4 copy-start.14
  429.1 3.8 copy-start.6
  432.9 1.8 copy-start.22
  434.7 1.8 copy-start.9
  437.1 3.1 copy-start.7
  447.5 6.4 copy-start.8
  456.0 5.4 copy-start.14
  461.4 3.8 copy-start.6
  672.7 5.2 copy-start.13
  672.7 9.3 %slice-start.2 = ((s8[4718592]{0:T(1024)(128)(4,1)}), s8[4194304]{0:T(1024)(128)(4,1)S(1)}, s32[]{:S(2)}) async-start(s8[4718592]{0:T(1024)(128)(4,1)} %bitcast.356), calls=%async_computation.6 | async-start | bytes 8388608
  677.9 3.2 copy-start.19
  677.9 4.0 slice-start.3
  681.1 4.0 slice-start
  682.0 3.5 slice-start.1
  685.5 2.2 copy-start.18
  (20 other events, 23.0 us)
Sparse Core Ops, SparseCore 0:
  39.8 65.0 all-gather.1
  199.6 137.7 reduce-scatter.1
  465.3 207.3 all-reduce.2
where the time goes:
time: 702 us; the launch traced here: 697 us
  matrix products  257 us (37%)
  waiting for transfers between devices  218 us (31%)
  other arithmetic  118 us (17%)
  local copies, waits for them, and re-layouts  52.3 us (7%)
  blocking collectives  32.8 us (5%)
  between operations  16.7 us (2%)
    psum x1, waiting for transfers between devices, local_step(): q_one, q_two, q_pgrad = lax.psum(q_grads, 'data')  174 us
    add x16, other arithmetic, body(): old_sum + new_part  86.5 us
    all_gather x1, waiting for transfers between devices, local_step(): all_docs = lax.all_gather(d_reps, 'data', axis=1, tiled=True)  40.7 us
    dot_general x16, matrix products, tower_backward(): lax.dot_general(h_in, pre_grad, ROWS_CONTRACT, preferred_element_type=jnp...  38.7 us
    dot_general x16, matrix products, tower_forward(): jnp.dot(act_bf, w_two[layer], preferred_element_type=jnp.float32)  37.9 us
    dot_general x24, matrix products, tower_forward(): pre_act = jnp.dot(hidden, w_one[layer], preferred_element_type=jnp.float32)  37.1 us
    psum x1, blocking collectives, local_step(): loss = lax.psum(jnp.sum(log_norm - pos_logit), 'data') / global_batch  32.8 us
    dot_general x1, matrix products, local_step(): lax.dot_general(q_reps, doc_flat, LAST_CONTRACT, preferred_element_type=j...  23.9 us
  transfers between devices with their start and end apart: 3, of which 3 were waited for; matrix products, arithmetic and copies ran while one was open for 22% of the time, Pallas kernels for 0%

commit v1 on v0

v1 whole, which is shorter than its diff:
```python
import functools

import jax
import jax.numpy as jnp
import numpy as np
from jax import lax
from jax.experimental import pallas as pl
from jax.experimental.pallas import tpu as pltpu
from jax.sharding import PartitionSpec as P

SUB_COUNT = 4
ND = 16
ROWS = 512
WIDTH = 384
FFN = 1536
BATCH = ROWS * ND
CHUNK = 2 * ROWS
BLOCKS = 17
HALF_ROWS = BLOCKS * WIDTH // 2
PART_ROWS = HALF_ROWS // 3
PIECE = PART_ROWS // 8
COLS = 512
MESH = pl.DeviceIdType.MESH
VMEM_MAX = 67_043_328
F32, BF16 = jnp.float32, jnp.bfloat16
K0 = float(np.sqrt(2.0 / np.pi).astype(np.float32))
LOW = -3.0e38
LOG2E = float(1.0 / np.log(2.0))

LAST = (((1,), (1,)), ((), ()))
FIRST = (((0,), (0,)), ((), ()))
NORMAL = (((1,), (0,)), ((), ()))


def mm(a, b, dims=NORMAL):
    return lax.dot_general(a, b, dims, preferred_element_type=F32)


def gelu(a):
    return a * (0.5 * (1.0 + jnp.tanh(K0 * (a + 0.044715 * (a * a * a)))))


def gelu_and_slope(a):
    sq = a * a
    t = jnp.tanh(K0 * (a + 0.044715 * (a * sq)))
    cdf = 0.5 * (1.0 + t)
    slope = cdf + a * (0.5 * (1.0 - t * t)) * (K0 + (3.0 * 0.044715 * K0) * sq)
    return a * cdf, slope


def forward_kernel(x_ref, w1_ref, w2_ref, p_ref, y_ref, u_ref):
    h = x_ref[...]
    for k in range(2):
        for c in range(FFN // COLS):
            cs = slice(c * COLS, (c + 1) * COLS)
            u_ref[:, cs] = gelu(mm(h, w1_ref[k, :, cs])).astype(BF16)
        h = (h.astype(F32) + mm(u_ref[...], w2_ref[k])).astype(BF16)
    y_ref[...] = mm(h, p_ref[...]).astype(BF16)


def tower_forward(rows, w1, w2, p):
    n = rows.shape[0]
    m = n // SUB_COUNT
    whole = lambda a: pl.BlockSpec(a.shape, lambda i: (0,) * a.ndim)
    return pl.pallas_call(
        forward_kernel,
        grid=(SUB_COUNT,),
        out_shape=jax.ShapeDtypeStruct((n, WIDTH), BF16),
        in_specs=[pl.BlockSpec((m, WIDTH), lambda i: (i, 0)), whole(w1), whole(w2), whole(p)],
        out_specs=pl.BlockSpec((m, WIDTH), lambda i: (i, 0)),
        scratch_shapes=[pltpu.VMEM((m, FFN), BF16)],
        compiler_params=pltpu.CompilerParams(vmem_limit_bytes=40 << 20),
        cost_estimate=pl.CostEstimate(flops=n * 5_000_000, bytes_accessed=n * 1536 + 5_000_000, transcendentals=0),
        name="tower_forward",
    )(rows, w1, w2, p)


def backward_kernel(x_ref, g_ref, w1_ref, w2_ref, p_ref, out_ref, u_ref, s_ref, h_ref, dl_ref):
    @pl.when(pl.program_id(0) == 0)
    def _():
        out_ref[...] = jnp.zeros_like(out_ref)

    h_ref[0] = x_ref[...]
    for k in range(2):
        h = h_ref[k]
        for c in range(FFN // COLS):
            cs = slice(c * COLS, (c + 1) * COLS)
            act, slope = gelu_and_slope(mm(h, w1_ref[k, :, cs]))
            u_ref[k, :, cs] = act.astype(BF16)
            s_ref[k, :, cs] = slope
        h_ref[k + 1] = (h.astype(F32) + mm(u_ref[k], w2_ref[k])).astype(BF16)
    g = g_ref[...]
    out_ref[16] += mm(h_ref[2], g, FIRST)
    e = mm(g, p_ref[...], LAST)
    for k in (1, 0):
        eb = e.astype(BF16)
        for c in range(4):
            out_ref[8 + 4 * k + c] += mm(u_ref[k, :, c * WIDTH:(c + 1) * WIDTH], eb, FIRST)
        for c in range(FFN // COLS):
            cs = slice(c * COLS, (c + 1) * COLS)
            dl_ref[:, cs] = (s_ref[k, :, cs] * mm(eb, w2_ref[k, cs, :], LAST)).astype(BF16)
        for c in range(2):
            part = mm(h_ref[k], dl_ref[:, 2 * c * WIDTH:2 * (c + 1) * WIDTH], FIRST)
            out_ref[4 * k + 2 * c] += part[:, :WIDTH]
            out_ref[4 * k + 2 * c + 1] += part[:, WIDTH:]
        if k == 1:
            e = e + mm(dl_ref[...], w1_ref[k], LAST)


def tower_backward(rows, up, w1, w2, p):
    n = rows.shape[0]
    m = n // SUB_COUNT
    whole = lambda a: pl.BlockSpec(a.shape, lambda i: (0,) * a.ndim)
    block = pl.BlockSpec((m, WIDTH), lambda i: (i, 0))
    return pl.pallas_call(
        backward_kernel,
        grid=(SUB_COUNT,),
        out_shape=jax.ShapeDtypeStruct((BLOCKS, WIDTH, WIDTH), F32),
        in_specs=[block, block, whole(w1), whole(w2), whole(p)],
        out_specs=pl.BlockSpec((BLOCKS, WIDTH, WIDTH), lambda i: (0, 0, 0)),
        scratch_shapes=[
            pltpu.VMEM((2, m, FFN), BF16),
            pltpu.VMEM((2, m, FFN), F32),
            pltpu.VMEM((3, m, WIDTH), BF16),
            pltpu.VMEM((m, FFN), BF16),
        ],
        compiler_params=pltpu.CompilerParams(vmem_limit_bytes=60 << 20),
        cost_estimate=pl.CostEstimate(flops=n * 15_000_000, bytes_accessed=n * 1536 + 15_000_000, transcendentals=0),
        name="tower_backward",
    )(rows, up, w1, w2, p)


def unpack(blocks):
    w1 = blocks[:8].reshape(2, 4, WIDTH, WIDTH).transpose(0, 2, 1, 3).reshape(2, WIDTH, FFN)
    return w1, blocks[8:16].reshape(2, FFN, WIDTH), blocks[16]


def bit_of(me, b):
    return lax.rem(me // (1 << b), 2)


def across(me, b):
    return me + (1 - 2 * bit_of(me, b)) * (1 << b)


def piece_rows(me, core, part, r):
    at = 0
    for i in range(3):
        bit = bit_of(me, 1 + (part + i) % 3)
        at = 2 * at + ((1 - bit) if (r >> (2 - i)) & 1 else bit)
    return pl.ds(pl.multiple_of(core * HALF_ROWS + part * PART_ROWS + at * PIECE, 8), PIECE)


def sum_kernel(x_ref, out_ref, acc, r0, r1, r2, r3, s0, s1, s2, s3, v0, v1, v2, v3, t0, t1, t2, t3, w0, w1, w2, w3):
    me = lax.axis_index("data")
    core = bit_of(me, 0)
    barrier = pltpu.get_barrier_semaphore()
    for b in range(4):
        pl.semaphore_signal(barrier, inc=1, device_id=(across(me, b),), device_id_type=MESH)
    pl.semaphore_wait(barrier, 4)

    def send(src, dst, send_sem, recv_sem, b):
        return pltpu.make_async_remote_copy(
            src_ref=src, dst_ref=dst, send_sem=send_sem, recv_sem=recv_sem,
            device_id=(across(me, b),), device_id_type=MESH)

    def mine(part, r):
        return piece_rows(me, core, part, r)

    def dim(part, i):
        return 1 + (part + i) % 3

    def swap(part, r):
        return send(x_ref.at[piece_rows(me, 1 - core, part, r)], r0.at[8 * part + r], s0.at[8 * part + r], v0.at[8 * part + r], 0)

    def first(part, r):
        return send(acc.at[8 * part + 4 + r], r1.at[4 * part + r], s1.at[4 * part + r], v1.at[4 * part + r], dim(part, 0))

    def second(part, r):
        return send(acc.at[8 * part + 2 + r], r2.at[2 * part + r], s2.at[2 * part + r], v2.at[2 * part + r], dim(part, 1))

    def third(part):
        return send(acc.at[8 * part + 1], r3.at[part], s3.at[part], v3.at[part], dim(part, 2))

    def back(part, r, level, theirs=False):
        if level == 3:
            where = piece_rows(me, 1 - core, part, r) if theirs else mine(part, r)
            k = 8 * part + r
            return send(out_ref.at[where], out_ref.at[where], t0.at[k], w0.at[k], 0)
        (ss, rs), n = (((t1, w1), 4), ((t2, w2), 2), ((t3, w3), 1))[level]
        where = mine(part, r + n) if theirs else mine(part, r)
        return send(out_ref.at[where], out_ref.at[where], ss.at[n * part + r], rs.at[n * part + r], dim(part, level))

    order = (7, 6, 5, 4, 3, 2, 1, 0)
    parts = range(3)
    for r in order:
        for p in parts:
            swap(p, r).start()
    for r in order:
        for p in parts:
            swap(p, r).wait_recv()
            acc[8 * p + r] = x_ref[mine(p, r), :] + r0[8 * p + r]
            if r >= 4:
                first(p, r - 4).start()
    for r in (3, 2):
        for p in parts:
            first(p, r).wait_recv()
            acc[8 * p + r] = acc[8 * p + r] + r1[4 * p + r]
            second(p, r - 2).start()
    for p in parts:
        first(p, 1).wait_recv()
        second(p, 1).wait_recv()
        acc[8 * p + 1] = acc[8 * p + 1] + r1[4 * p + 1] + r2[2 * p + 1]
        third(p).start()
    for p in parts:
        first(p, 0).wait_recv()
        second(p, 0).wait_recv()
        acc[8 * p] = acc[8 * p] + r1[4 * p] + r2[2 * p]
    for p in parts:
        third(p).wait_recv()
        out_ref[mine(p, 0), :] = acc[8 * p] + r3[p]
        back(p, 0, 2).start()
    for level in (1, 0, 3):
        for p in parts:
            back(p, 0, level).start()
    for p in parts:
        back(p, 0, 2, True).wait_recv()
        back(p, 1, 1).start()
    for p in parts:
        back(p, 1, 0).start()
        back(p, 1, 3).start()
    for r in (0, 1):
        for p in parts:
            back(p, r, 1, True).wait_recv()
            back(p, 2 + r, 0).start()
            back(p, 2 + r, 3).start()
    for r in range(4):
        for p in parts:
            back(p, r, 0, True).wait_recv()
            back(p, 4 + r, 3).start()
    for r in range(8):
        for p in parts:
            back(p, r, 3, True).wait_recv()
    for p in parts:
        for r in range(8):
            swap(p, r).wait_send()
            back(p, r, 3).wait_send()
        for r in range(4):
            first(p, r).wait_send()
            back(p, r, 0).wait_send()
        for r in range(2):
            second(p, r).wait_send()
            back(p, r, 1).wait_send()
        third(p).wait_send()
        back(p, 0, 2).wait_send()


def sum_devices(blocks):
    x = blocks.reshape(BLOCKS * WIDTH, WIDTH)
    vmem = pl.BlockSpec(memory_space=pltpu.VMEM)
    counts = (24, 12, 6, 3)
    out = pl.pallas_call(
        sum_kernel,
        out_shape=jax.ShapeDtypeStruct(x.shape, F32),
        in_specs=[vmem],
        out_specs=vmem,
        scratch_shapes=[pltpu.VMEM((24, PIECE, WIDTH), F32)]
        + [pltpu.VMEM((n, PIECE, WIDTH), F32) for n in counts]
        + [pltpu.SemaphoreType.DMA((n,)) for n in counts * 4],
        compiler_params=pltpu.CompilerParams(collective_id=1, has_side_effects=True, vmem_limit_bytes=60 << 20),
        name="sum_devices",
    )(x)
    return out.reshape(blocks.shape)


def gather_kernel(tau_ref, docs_own, x_ref, w1_ref, w2_ref, p_ref, up_ref, stat_ref, q_all, docs, e_ref, m_ref, g_ref, acc, u_ref,
                  q_ref, mine_ref, *sems):
    me = lax.axis_index("data")
    d_sems, q_sems, (share_send, share_recv, local_sem) = sems[:8], sems[8:16], sems[16:]
    inv_tau = 1.0 / tau_ref[0]
    c = inv_tau * LOG2E
    scale = inv_tau / BATCH
    parts = range(3)

    barrier = pltpu.get_barrier_semaphore()
    for p in range(1, ND):
        pl.semaphore_signal(barrier, inc=1, device_id=(lax.rem(me + p, ND),), device_id_type=MESH)
    pl.semaphore_wait(barrier, ND - 1)

    def place(part, r, other=0):
        dev = across(me, 0) if other else me
        for i in range(3):
            if (r >> (2 - i)) & 1:
                dev = dev + (1 - 2 * bit_of(me, 1 + (part + i) % 3)) * (1 << (1 + (part + i) % 3))
        return dev

    def hop(own, everyone, cuts, sem, part, r, level, theirs=False):
        n = (4, 2, 1, 8)[level]
        ss, rs = sem[2 * level], sem[2 * level + 1]
        rows, lo, hi = own.shape[0], cuts[part], cuts[part + 1]

        def at(dev):
            return pl.ds(pl.multiple_of(dev * rows + lo, 16), hi - lo)

        if theirs:
            src = dst = everyone.at[at(place(part, r, 1) if level == 3 else place(part, r + n))]
        else:
            dst = everyone.at[at(place(part, r))]
            src = own.at[pl.ds(lo, hi - lo)] if r == 0 else dst
        return pltpu.make_async_remote_copy(
            src_ref=src, dst_ref=dst, send_sem=ss.at[n * part + r], recv_sem=rs.at[n * part + r],
            device_id=(across(me, 0 if level == 3 else 1 + (part + level) % 3),), device_id_type=MESH)

    doc = functools.partial(hop, docs_own, docs, (0, 336, 672, 1024), d_sems)
    qry = functools.partial(hop, q_ref, q_all, (0, 176, 352, 512), q_sems)

    def begin(f):
        for level in (2, 1, 0, 3):
            for p in parts:
                f(p, 0, level).start()

    def tick_one(f):
        for p in parts:
            f(p, 0, 2, True).wait_recv()
            f(p, 1, 1).start()
        for p in parts:
            f(p, 1, 0).start()
            f(p, 1, 3).start()

    def tick_two(f, r):
        for p in parts:
            f(p, r, 1, True).wait_recv()
            f(p, 2 + r, 0).start()
            f(p, 2 + r, 3).start()

    def tick_last(f, rs):
        for r in rs:
            for p in parts:
                f(p, r, 0, True).wait_recv()
                f(p, 4 + r, 3).start()

    def tick_core(f, rs):
        for r in rs:
            for p in parts:
                f(p, r, 3, True).wait_recv()

    def drain(f):
        for p in parts:
            for level, n in ((0, 4), (1, 2), (2, 1), (3, 8)):
                for r in range(n):
                    f(p, r, level).wait_send()

    begin(doc)
    docs[pl.ds(pl.multiple_of(me * CHUNK, CHUNK), CHUNK), :] = docs_own[...]
    m = ROWS // SUB_COUNT

    def forward(i, _):
        at = pl.ds(pl.multiple_of(i * m, m), m)
        h = x_ref[at, :]
        for k in range(2):
            for j in range(FFN // COLS):
                cs = slice(j * COLS, (j + 1) * COLS)
                u_ref[:, cs] = gelu(mm(h, w1_ref[k, :, cs])).astype(BF16)
            h = (h.astype(F32) + mm(u_ref[...], w2_ref[k])).astype(BF16)
        q_ref[at, :] = mm(h, p_ref[...]).astype(BF16)
        return 0

    lax.fori_loop(0, SUB_COUNT, forward, 0)
    local = pltpu.make_async_copy(q_ref, q_all.at[pl.ds(pl.multiple_of(me * ROWS, ROWS), ROWS)], local_sem)
    local.start()
    tick_one(doc)
    m_ref[...] = jnp.full_like(m_ref, LOW)
    lane = lax.broadcasted_iota(jnp.int32, (ROWS, 128), 1)

    def device_at(k):
        chip = k // 2
        chip = jnp.where(chip == 3, 4, jnp.where(chip == 4, 3, chip))
        flips = 2 * chip + lax.rem(k, 2)
        return me + sum((1 - 2 * bit_of(me, b)) * (1 << b) * lax.rem(flips // (1 << b), 2) for b in range(4))

    def score(k, carry):
        @pl.when(k == 1)
        def _():
            tick_core(doc, (0,))

        @pl.when(k == 2)
        def _():
            tick_two(doc, 0)
            tick_last(doc, (0,))

        @pl.when(k == 3)
        def _():
            tick_core(doc, (1, 2, 4))

        @pl.when(k == 8)
        def _():
            tick_two(doc, 1)
            begin(qry)
            tick_last(doc, (1, 2))

        @pl.when(k == 9)
        def _():
            tick_core(doc, (3, 5, 6))

        @pl.when(k == 14)
        def _():
            tick_last(doc, (3,))

        @pl.when(k == 15)
        def _():
            tick_core(doc, (7,))

        top, total = carry
        base = device_at(k) * CHUNK
        marks = m_ref[...]
        for half in range(2):
            rows = docs[pl.ds(pl.multiple_of(base + half * ROWS, ROWS), ROWS), :]
            s = mm(q_ref[...], rows, LAST)
            best = jnp.max(s, axis=1, keepdims=True)
            e = jnp.exp2((s - best) * c)
            e_ref[k, :, half * ROWS:(half + 1) * ROWS] = e
            marks = jnp.where(lane == 2 * k + half, best, marks)
            new_top = jnp.maximum(top, best)
            total = total * jnp.exp2((top - new_top) * c) + jnp.sum(e, axis=1, keepdims=True) * jnp.exp2((best - new_top) * c)
            top = new_top
        m_ref[...] = marks
        return top, total

    top, total = lax.fori_loop(0, ND, score, (jnp.full((ROWS, 1), LOW, F32), jnp.zeros((ROWS, 1), F32)))
    pos = jnp.sum(q_ref[...].astype(F32) * docs_own[0:ROWS, :].astype(F32), axis=1, keepdims=True)
    loss = (top - pos) * inv_tau + jnp.log(total)
    weight = scale / total
    mine_ref[...] = jnp.where(lane == 0, top, jnp.where(lane == 1, weight, loss)).T[0:8, :]
    stat_ref[me] = mine_ref[...]

    def share(p, slot):
        return pltpu.make_async_remote_copy(
            src_ref=mine_ref, dst_ref=stat_ref.at[slot], send_sem=share_send.at[p], recv_sem=share_recv.at[p],
            device_id=(lax.rem(me + p, ND),), device_id_type=MESH)

    for p in range(1, ND):
        share(p, me).start()
    m_ref[...] = jnp.exp2((m_ref[...] - top) * c) * weight
    tick_one(qry)

    def weighted(k, half):
        f = jnp.sum(jnp.where(lane == 2 * k + half, m_ref[...], 0.0), axis=1, keepdims=True)
        return e_ref[k, :, half * ROWS:(half + 1) * ROWS] * f

    r = lax.broadcasted_iota(jnp.int32, (ROWS, ROWS), 0)
    col = lax.broadcasted_iota(jnp.int32, (ROWS, ROWS), 1)
    acc[...] = mm((weighted(0, 0) - jnp.where(r == col, scale, 0.0)).astype(BF16), docs_own[0:ROWS, :])
    acc[...] += mm(weighted(0, 1).astype(BF16), docs_own[ROWS:, :])

    def pull(k, _):
        @pl.when(k == 5)
        def _():
            tick_two(qry, 0)
            tick_last(qry, (0,))

        @pl.when(k == 10)
        def _():
            tick_two(qry, 1)

        base = device_at(k) * CHUNK
        for half in range(2):
            g_ref[:, half * ROWS:(half + 1) * ROWS] = weighted(k, half).astype(BF16)
        acc[...] += mm(g_ref[...], docs[pl.ds(pl.multiple_of(base, CHUNK), CHUNK), :])
        return 0

    lax.fori_loop(1, ND, pull, 0)
    up_ref[...] = acc[...].astype(BF16)
    tick_last(qry, (1, 2, 3))
    tick_core(qry, range(8))
    for p in range(1, ND):
        share(p, me).wait_send()
        share(p, lax.rem(me + ND - p, ND)).wait_recv()
    drain(doc)
    drain(qry)
    local.wait()


def gather_rows(tau, docs_own, x, w1, w2, p):
    vmem = pl.BlockSpec(memory_space=pltpu.VMEM)
    hops = [pltpu.SemaphoreType.DMA((3 * n,)) for n in (4, 4, 2, 2, 1, 1, 8, 8)]
    return pl.pallas_call(
        gather_kernel,
        out_shape=[
            jax.ShapeDtypeStruct((ROWS, WIDTH), BF16),
            jax.ShapeDtypeStruct((ND, 8, ROWS), F32),
            jax.ShapeDtypeStruct((BATCH, WIDTH), BF16),
        ],
        in_specs=[pl.BlockSpec(memory_space=pltpu.SMEM)] + [vmem] * 5,
        out_specs=[vmem, vmem, pl.BlockSpec(memory_space=pl.ANY)],
        scratch_shapes=[
            pltpu.VMEM((2 * BATCH, WIDTH), BF16),
            pltpu.VMEM((ND, ROWS, CHUNK), F32),
            pltpu.VMEM((ROWS, 128), F32),
            pltpu.VMEM((ROWS, CHUNK), BF16),
            pltpu.VMEM((ROWS, WIDTH), F32),
            pltpu.VMEM((ROWS // SUB_COUNT, FFN), BF16),
            pltpu.VMEM((ROWS, WIDTH), BF16),
            pltpu.VMEM((8, ROWS), F32),
        ] + hops + hops + [pltpu.SemaphoreType.DMA((ND,)), pltpu.SemaphoreType.DMA((ND,)), pltpu.SemaphoreType.DMA],
        compiler_params=pltpu.CompilerParams(collective_id=0, has_side_effects=True, vmem_limit_bytes=VMEM_MAX),
        cost_estimate=pl.CostEstimate(flops=15_000_000_000, bytes_accessed=14_000_000, transcendentals=0),
        name="gather_rows",
    )(tau, docs_own, x, w1, w2, p)


def col_kernel(tau_ref, stat_ref, own_ref, q_ref, up_ref, q_all, g_ref, acc, sems):
    me = lax.axis_index("data")
    inv_tau = 1.0 / tau_ref[0]
    c = inv_tau * LOG2E
    scale = inv_tau / BATCH

    def rows_of(k):
        return pl.ds(pl.multiple_of(lax.rem(me + k, ND) * ROWS, ROWS), ROWS)

    def chunk_copy(k):
        return pltpu.make_async_copy(q_ref.at[rows_of(k)], q_all.at[rows_of(k)], sems.at[k])

    for k in range(ND):
        chunk_copy(k).start()

    def probs(k):
        j = lax.rem(me + k, ND)
        s = mm(own_ref[...], q_all[rows_of(k), :], LAST)
        return jnp.exp2((s - stat_ref[j, 0:1, :]) * c) * stat_ref[j, 1:2, :]

    chunk_copy(0).wait()
    prob = probs(0)
    r = lax.broadcasted_iota(jnp.int32, (CHUNK, ROWS), 0)
    col = lax.broadcasted_iota(jnp.int32, (CHUNK, ROWS), 1)
    acc[...] = mm((prob - jnp.where(r == col, scale, 0.0)).astype(BF16), q_all[rows_of(0), :])

    def step(i, _):
        for n in range(3):
            k = 3 * i + n + 1
            chunk_copy(k).wait()
            g_ref[n] = probs(k).astype(BF16)
            acc[...] += mm(g_ref[n], q_all[rows_of(k), :])
        return 0

    lax.fori_loop(0, 5, step, 0)
    up_ref[...] = acc[...].astype(BF16)


def loss_cols(tau, stats, own, q_all):
    vmem = pl.BlockSpec(memory_space=pltpu.VMEM)
    return pl.pallas_call(
        col_kernel,
        out_shape=jax.ShapeDtypeStruct((CHUNK, WIDTH), BF16),
        in_specs=[pl.BlockSpec(memory_space=pltpu.SMEM), vmem, vmem, pl.BlockSpec(memory_space=pl.ANY)],
        out_specs=vmem,
        scratch_shapes=[
            pltpu.VMEM((BATCH, WIDTH), BF16),
            pltpu.VMEM((3, CHUNK, ROWS), BF16),
            pltpu.VMEM((CHUNK, WIDTH), F32),
            pltpu.SemaphoreType.DMA((ND,)),
        ],
        compiler_params=pltpu.CompilerParams(vmem_limit_bytes=60 << 20),
        cost_estimate=pl.CostEstimate(flops=13_000_000_000, bytes_accessed=8_000_000, transcendentals=0),
        name="loss_cols",
    )(tau, stats, own, q_all)


def local_step(q_loc, d_loc, temperature, q_w1, q_w2, q_proj, d_w1, d_w2, d_proj):
    tau = temperature.reshape(1)
    d_rows = d_loc.reshape(CHUNK, WIDTH)
    d_reps = tower_forward(d_rows, d_w1, d_w2, d_proj)
    q_up, stats, q_all = gather_rows(tau, d_reps, q_loc, q_w1, q_w2, q_proj)
    loss = jnp.sum(stats[:, 2, :]) / BATCH
    q_grads = tower_backward(q_loc, q_up, q_w1, q_w2, q_proj)
    q_sum = lax.psum(q_grads, "data")
    stats, q_grads = lax.optimization_barrier((stats, q_grads))
    d_up = loss_cols(tau, stats, d_reps, q_all)
    d_sum = sum_devices(tower_backward(d_rows, d_up, d_w1, d_w2, d_proj))
    return (loss, *unpack(q_sum), *unpack(d_sum))


def solution(mesh):
    specs_in = (P("data", None), P(None, "data", None), P(), P(), P(), P(), P(), P(), P())
    specs_out = (P(), P(), P(), P(), P(), P(), P())
    return jax.shard_map(local_step, mesh=mesh, in_specs=specs_in, out_specs=specs_out, check_vma=False)
```

time: 702 us -> 330 us (0.47)
  Pallas kernels: 0 us -> 283 us
  matrix products: 257 us -> 0 us
  waiting for transfers between devices: 218 us -> 0.04 us
  other arithmetic: 118 us -> 1.62 us
  blocking collectives: 32.8 us -> 0 us
  local copies, waits for them, and re-layouts: 52.3 us -> 28.9 us
    pallas_call x0 -> x6, Pallas kernels: none -> 283 us  [the longest x1 121 us: sum_devices(): pl.pallas_call(sum_kernel, out_shape=jax.ShapeDtypeStruct(x.shape, F32),...]
    dot_general x115 -> x0, matrix products: 257 us -> none  [the longest x16 38.7 us: tower_backward(): lax.dot_general(h_in, pre_grad, ROWS_CONTRACT, preferred_element_type=jnp...]
    psum x1, waiting for transfers between devices: 174 us -> 0.02 us  [local_step(): q_sum = lax.psum(q_grads, 'data')]
    add x17 -> x0, other arithmetic: 86.5 us -> none  [the longest x16 86.5 us: body(): old_sum + new_part]
    all_gather x1 -> x0, waiting for transfers between devices: 40.7 us -> none  [local_step(): all_docs = lax.all_gather(d_reps, 'data', axis=1, tiled=True)]
    psum x1 -> x0, blocking collectives: 32.8 us -> none  [local_step(): loss = lax.psum(jnp.sum(log_norm - pos_logit), 'data') / global_batch]
    dot_general x1 -> x0, local copies, waits for them, and re-layouts: 22.5 us -> none  [local_step(): lax.dot_general(grad_logit, q_reps, ROWS_CONTRACT, preferred_element_type...]
    reduce_sum x2 -> x1, other arithmetic: 17.9 us -> 1.62 us  [local_step(): loss = jnp.sum(stats[:, 2, :]) / BATCH]
  transfers between devices with their start and end apart: 3 -> 1, of which waited for: 3 -> 0; matrix products, arithmetic and copies ran while one was open for 22% -> 4% of each run, Pallas kernels for 0% -> 53%
where the time goes in v1:
time: 330 us
  Pallas kernels  283 us (86%)
  local copies, waits for them, and re-layouts  28.9 us (9%)
  between operations  16.5 us (5%)
    pallas_call x1, Pallas kernels, sum_devices(): pl.pallas_call(sum_kernel, out_shape=jax.ShapeDtypeStruct(x.shape, F32),...  121 us
    pallas_call x1, Pallas kernels, gather_rows(): pl.pallas_call(gather_kernel, out_shape=[jax.ShapeDtypeStruct((ROWS, WIDT...  75.5 us
    pallas_call x2, Pallas kernels, tower_backward(): pl.pallas_call(backward_kernel, grid=(SUB_COUNT,), out_shape=jax.ShapeDty...  54 us
    pallas_call x1, Pallas kernels, loss_cols(): pl.pallas_call(col_kernel, out_shape=jax.ShapeDtypeStruct((CHUNK, WIDTH),...  23.9 us
    slice x3, local copies, waits for them, and re-layouts, unpack(): return (w1, blocks[8:16].reshape(2, FFN, WIDTH), blocks[16])  15.1 us
    pallas_call x1, Pallas kernels, tower_forward(): pl.pallas_call(forward_kernel, grid=(SUB_COUNT,), out_shape=jax.ShapeDtyp...  8.7 us
  transfers between devices with their start and end apart: 1, of which 0 were waited for; matrix products, arithmetic and copies ran while one was open for 4% of the time, Pallas kernels for 53%

profile of v1, /device:TPU:0, one launch (start us, length us, event | category | flops | bytes accessed | tf_op | source)
XLA Modules:
  0.0 329.9 jit_solution(10701200748465964796)
XLA Ops:
  7.2 0.0 all-reduce.2.cloned.1.call-start
  7.9 0.0 copy-start
  7.9 1.7 copy-done
  9.5 0.0 copy-start.1
  9.5 1.7 copy-done.1
  11.2 0.0 copy-start.2
  11.2 1.1 copy-done.2
  12.3 0.0 copy-start.3
  12.3 1.0 copy-done.3
  13.3 8.7 %tower_forward.1.docs_own.own_ref = bf16[1024,384]{1,0:T(8,128)(2,1)S(1)} custom-call(bf16[1024,384]{1,0:T(8,128)(2,1)S(1)} %bitcast.20, bf16[2,384,1536]{2,1,0:T(8,128)(2,1)S(1)} %copy-done, bf16[2,1536,384]{2,1,0:T(8,128)(2,1)S(1)} %copy-done.1, bf16[384,384]{1,0:T(8,128)(2,1)S(1)} %copy-done.3), custom_call_target="tpu_custom_call" | custom-call | flops 5120000000 | bytes 6572864 | tf_op jit(solution)/shard_map/tower_forward/pallas_call | solution.py:65
  22.0 0.0 copy-start.4
  22.0 0.9 copy-done.4
  22.9 75.5 %gather_rows.1 = (bf16[512,384]{1,0:T(8,128)(2,1)}, f32[16,8,512]{2,1,0:T(8,128)}, bf16[8192,384]{1,0:T(8,128)(2,1)}) custom-call(f32[1]{0:T(128)} %bitcast.17.tau_ref, bf16[1024,384]{1,0:T(8,128)(2,1)} %copy-done.4, bf16[512,384]{1,0:T(8,128)(2,1)} %x_ref.3, bf16[2,384,1536]{2,1,0:T(8,128)(2,1)} %w1_ref.6, bf16[2,1536,384]{2,1,0:T(8,128)(2,1)} %w2_ref.6, ...), custom_call_target="tpu_custom_call" | custom-call | flops 15000000512 | bytes 14000000 | tf_op jit(solution)/shard_map/gather_rows/pallas_call | solution.py:486
  98.4 24.2 %tower_backward.2 = f32[17,384,384]{2,1,0:T(8,128)} custom-call(bf16[512,384]{1,0:T(8,128)(2,1)} %x_ref.3, bf16[512,384]{1,0:T(8,128)(2,1)} %get-tuple-element.12.g_ref, bf16[2,384,1536]{2,1,0:T(8,128)(2,1)} %w1_ref.6, bf16[2,1536,384]{2,1,0:T(8,128)(2,1)} %w2_ref.6, bf16[384,384]{1,0:T(8,128)(2,1)} %p_ref.6), custom_call_target="tpu_custom_call" | custom-call | flops 7680000000 | bytes 15786432 | tf_op jit(solution)/shard_map/tower_backward/pallas_call | solution.py:115
  122.5 0.0 all-reduce.2.cloned.1.call-update
  122.6 23.9 %loss_cols.1.g_ref = bf16[1024,384]{1,0:T(8,128)(2,1)} custom-call(f32[1]{0:T(128)} %bitcast.18.tau_ref, f32[16,8,512]{2,1,0:T(8,128)} %get-tuple-element.13.stat_ref, bf16[1024,384]{1,0:T(8,128)(2,1)} %copy-done.4, bf16[8192,384]{1,0:T(8,128)(2,1)} %get-tuple-element.14.q_ref), custom_call_target="tpu_custom_call" | custom-call | flops 12999999488 | bytes 8000000 | tf_op jit(solution)/shard_map/loss_cols/pallas_call | solution.py:551
  146.5 29.8 %tower_backward.3 = f32[17,384,384]{2,1,0:T(8,128)} custom-call(bf16[1024,384]{1,0:T(8,128)(2,1)} %bitcast.19, bf16[1024,384]{1,0:T(8,128)(2,1)} %loss_cols.1.g_ref, bf16[2,384,1536]{2,1,0:T(8,128)(2,1)} %w1_ref.7, bf16[2,1536,384]{2,1,0:T(8,128)(2,1)} %w2_ref.7, bf16[384,384]{1,0:T(8,128)(2,1)} %p_ref.7), custom_call_target="tpu_custom_call" | custom-call | flops 15360000000 | bytes 16572864 | tf_op jit(solution)/shard_map/tower_backward/pallas_call | solution.py:115
  176.3 120.8 %sum_devices.1 = f32[6528,384]{1,0:T(8,128)} custom-call(f32[6528,384]{1,0:T(8,128)} %bitcast.23), custom_call_target="tpu_custom_call" | custom-call | tf_op jit(solution)/shard_map/sum_devices/pallas_call | solution.py:262
  297.0 1.9 slice.30
  298.9 6.6 %fusion = (f32[3072,384]{1,0:T(8,128)}, f32[3072,384]{1,0:T(8,128)S(1)}) fusion(f32[6528,384]{1,0:T(8,128)} %sum_devices.1), kind=kLoop, calls=%fused_computation.2 | loop fusion | bytes 18874368 | tf_op jit(solution)/shard_map/slice | solution.py:135
  305.5 2.8 copy.19
  308.3 1.6 slice_reduce_fusion
  310.6 0.0 all-reduce.2.cloned.1.call-done
  310.6 6.6 %fusion.1 = (f32[8,384,384]{2,1,0:T(8,128)}, f32[8,384,384]{2,1,0:T(8,128)S(1)}) fusion(f32[17,384,384]{2,1,0:T(8,128)} %all-reduce.2.cloned.1.call-done), kind=kLoop, calls=%fused_computation.3 | loop fusion | bytes 18874368 | tf_op jit(solution)/shard_map/slice | solution.py:135
  317.2 2.8 copy.18
  320.1 1.9 slice_bitcast_fusion
Async XLA Ops:
  7.2 303.5 %all-reduce.2.cloned.1.call-start = ((), (), s32[]{:S(2)}) async-start(), calls=%async_computation | async-start | bytes 20054016 | tf_op jit(solution)/shard_map/psum | solution.py:575
  7.9 1.7 copy-start
  9.5 1.7 copy-start.1
  11.2 1.1 copy-start.2
  12.3 1.0 copy-start.3
  22.0 0.9 copy-start.4
Sparse Core Ops, SparseCore 0:
  122.7 164.5 all-reduce.1

commit v2 on v1

v2 whole, which is shorter than its diff:
```python
import functools

import jax
import jax.numpy as jnp
import numpy as np
from jax import lax
from jax.experimental import pallas as pl
from jax.experimental.pallas import tpu as pltpu
from jax.sharding import PartitionSpec as P

SUB_COUNT = 4
ND = 16
ROWS = 512
WIDTH = 384
FFN = 1536
BATCH = ROWS * ND
CHUNK = 2 * ROWS
BLOCKS = 17
HALF_ROWS = BLOCKS * WIDTH // 2
PART_ROWS = HALF_ROWS // 3
PIECE = PART_ROWS // 8
PARTS = range(3)
NEAR, FAR = range(3, -1, -1), range(7, 3, -1)
HOPS = (4, 2, 1, 8)
COLS = 512
TILES = range(FFN // COLS)
MESH = pl.DeviceIdType.MESH
VMEM_MAX = 67_043_328
F32, BF16 = jnp.float32, jnp.bfloat16
K0 = float(np.sqrt(2.0 / np.pi).astype(np.float32))
LOW = -3.0e38
LOG2E = float(1.0 / np.log(2.0))

LAST = (((1,), (1,)), ((), ()))
FIRST = (((0,), (0,)), ((), ()))
NORMAL = (((1,), (0,)), ((), ()))


def mm(a, b, dims=NORMAL):
    return lax.dot_general(a, b, dims, preferred_element_type=F32)


def gelu(a):
    return a * (0.5 * (1.0 + jnp.tanh(K0 * (a + 0.044715 * (a * a * a)))))


def gelu_and_slope(a):
    sq = a * a
    t = jnp.tanh(K0 * (a + 0.044715 * (a * sq)))
    cdf = 0.5 * (1.0 + t)
    slope = cdf + a * (0.5 * (1.0 - t * t)) * (K0 + (3.0 * 0.044715 * K0) * sq)
    return a * cdf, slope


def forward_kernel(x_ref, w1_ref, w2_ref, p_ref, y_ref, u_ref):
    h = x_ref[...]
    for k in range(2):
        for c in TILES:
            cs = slice(c * COLS, (c + 1) * COLS)
            u_ref[:, cs] = gelu(mm(h, w1_ref[k, :, cs])).astype(BF16)
        h = (h.astype(F32) + mm(u_ref[...], w2_ref[k])).astype(BF16)
    y_ref[...] = mm(h, p_ref[...]).astype(BF16)


def tower_forward(rows, w1, w2, p):
    n = rows.shape[0]
    m = n // SUB_COUNT
    whole = lambda a: pl.BlockSpec(a.shape, lambda i: (0,) * a.ndim)
    return pl.pallas_call(
        forward_kernel,
        grid=(SUB_COUNT,),
        out_shape=jax.ShapeDtypeStruct((n, WIDTH), BF16),
        in_specs=[pl.BlockSpec((m, WIDTH), lambda i: (i, 0)), whole(w1), whole(w2), whole(p)],
        out_specs=pl.BlockSpec((m, WIDTH), lambda i: (i, 0)),
        scratch_shapes=[pltpu.VMEM((m, FFN), BF16)],
        compiler_params=pltpu.CompilerParams(vmem_limit_bytes=40 << 20),
        name="tower_forward",
    )(rows, w1, w2, p)


def backward_rows(x, g, w1_ref, w2_ref, p_ref, add, u_ref, s_ref, h_ref, dl_ref, middle=None):
    h_ref[0] = x
    for k in range(2):
        h = h_ref[k]
        for c in TILES:
            cs = slice(c * COLS, (c + 1) * COLS)
            act, slope = gelu_and_slope(mm(h, w1_ref[k, :, cs]))
            u_ref[k, :, cs] = act.astype(BF16)
            s_ref[k, :, cs] = slope
        h_ref[k + 1] = (h.astype(F32) + mm(u_ref[k], w2_ref[k])).astype(BF16)
    if middle is not None:
        middle()
    add(16, mm(h_ref[2], g, FIRST))
    e = mm(g, p_ref[...], LAST)
    for k in (1, 0):
        eb = e.astype(BF16)
        for c in range(4):
            add(8 + 4 * k + c, mm(u_ref[k, :, c * WIDTH:(c + 1) * WIDTH], eb, FIRST))
        for c in TILES:
            cs = slice(c * COLS, (c + 1) * COLS)
            dl_ref[:, cs] = (s_ref[k, :, cs] * mm(eb, w2_ref[k, cs, :], LAST)).astype(BF16)
        for c in range(2):
            part = mm(h_ref[k], dl_ref[:, 2 * c * WIDTH:2 * (c + 1) * WIDTH], FIRST)
            add(4 * k + 2 * c, part[:, :WIDTH])
            add(4 * k + 2 * c + 1, part[:, WIDTH:])
        if k == 1:
            e = e + mm(dl_ref[...], w1_ref[k], LAST)


def backward_kernel(x_ref, g_ref, w1_ref, w2_ref, p_ref, out_ref, u_ref, s_ref, h_ref, dl_ref):
    @pl.when(pl.program_id(0) == 0)
    def _():
        out_ref[...] = jnp.zeros_like(out_ref)

    def add(block, value):
        out_ref[block] += value

    backward_rows(x_ref[...], g_ref[...], w1_ref, w2_ref, p_ref, add, u_ref, s_ref, h_ref, dl_ref)


def tower_backward(rows, up, w1, w2, p):
    n = rows.shape[0]
    m = n // SUB_COUNT
    whole = lambda a: pl.BlockSpec(a.shape, lambda i: (0,) * a.ndim)
    block = pl.BlockSpec((m, WIDTH), lambda i: (i, 0))
    return pl.pallas_call(
        backward_kernel,
        grid=(SUB_COUNT,),
        out_shape=jax.ShapeDtypeStruct((BLOCKS, WIDTH, WIDTH), F32),
        in_specs=[block, block, whole(w1), whole(w2), whole(p)],
        out_specs=pl.BlockSpec((BLOCKS, WIDTH, WIDTH), lambda i: (0, 0, 0)),
        scratch_shapes=[
            pltpu.VMEM((2, m, FFN), BF16),
            pltpu.VMEM((2, m, FFN), F32),
            pltpu.VMEM((3, m, WIDTH), BF16),
            pltpu.VMEM((m, FFN), BF16),
        ],
        compiler_params=pltpu.CompilerParams(vmem_limit_bytes=60 << 20),
        name="tower_backward",
    )(rows, up, w1, w2, p)


def unpack_kernel(q_ref, d_ref, *refs):
    outs, hold, load, store = refs[:6], refs[6], refs[7], refs[8]

    def place(j):
        w1, w2, p = outs[3 * (j // BLOCKS):3 * (j // BLOCKS) + 3]
        n = j % BLOCKS
        if n < 8:
            return w1.at[n // 4, :, pl.ds(n % 4 * WIDTH, WIDTH)]
        if n < 16:
            return w2.at[(n - 8) // 4, pl.ds(n % 4 * WIDTH, WIDTH), :]
        return p

    def fetch(j):
        return pltpu.make_async_copy((q_ref, d_ref)[j // BLOCKS].at[j % BLOCKS], hold.at[j], load.at[j])

    def put(j):
        return pltpu.make_async_copy(hold.at[j], place(j), store.at[j])

    for j in range(2 * BLOCKS):
        fetch(j).start()
    for j in range(2 * BLOCKS):
        fetch(j).wait()
        put(j).start()
    for j in range(2 * BLOCKS):
        put(j).wait()


def unpack(q_blocks, d_blocks, shapes):
    hbm = pl.BlockSpec(memory_space=pl.ANY)
    return pl.pallas_call(
        unpack_kernel,
        out_shape=[jax.ShapeDtypeStruct(a, F32) for a in shapes],
        in_specs=[hbm, hbm],
        out_specs=[hbm] * 6,
        scratch_shapes=[
            pltpu.VMEM((2 * BLOCKS, WIDTH, WIDTH), F32),
            pltpu.SemaphoreType.DMA((2 * BLOCKS,)),
            pltpu.SemaphoreType.DMA((2 * BLOCKS,)),
        ],
        compiler_params=pltpu.CompilerParams(vmem_limit_bytes=24 << 20),
        name="unpack",
    )(q_blocks, d_blocks)


def bit_of(me, b):
    return lax.rem(me // (1 << b), 2)


def across(me, b):
    return me + (1 - 2 * bit_of(me, b)) * (1 << b)


def sum_places(me):
    core, bits = bit_of(me, 0), [bit_of(me, b) for b in (1, 2, 3)]
    mine, partner = [], []
    for p in PARTS:
        side = [(bits[(p + i) % 3] * (4 >> i) * PIECE, (1 - bits[(p + i) % 3]) * (4 >> i) * PIECE) for i in range(3)]
        for r in range(8):
            at = p * PART_ROWS + side[0][r >> 2] + side[1][(r >> 1) & 1] + side[2][r & 1]
            mine.append(pl.ds(pl.multiple_of(core * HALF_ROWS + at, 8), PIECE))
            partner.append(pl.ds(pl.multiple_of((1 - core) * HALF_ROWS + at, 8), PIECE))
    return mine, partner, [across(me, b) for b in range(4)]


class Gather:
    def __init__(self, copy):
        self.copy = copy

    def begin(self):
        for level in (2, 1, 0, 3):
            for p in PARTS:
                self.copy(p, 0, level).start()

    def pass_on(self, level, *rs):
        for r in rs:
            for p in PARTS:
                self.copy(p, r, level, True).wait_recv()
                for lower in (*range(level - 1, -1, -1), 3):
                    self.copy(p, r + HOPS[level], lower).start()

    def core(self, *rs):
        for r in rs:
            for p in PARTS:
                self.copy(p, r, 3, True).wait_recv()

    def drain(self):
        for level, n in enumerate(HOPS):
            for r in range(n):
                for p in PARTS:
                    self.copy(p, r, level).wait_send()


HOP_SEMS = [pltpu.SemaphoreType.DMA((3 * n,)) for n in HOPS for _ in range(2)]


class DeviceSum:
    def __init__(self, places, own, other, out, bufs, sems, load=None):
        self.mine, self.partner, self.peers = places
        self.own, self.other, self.out, self.load = own, other, out, load
        self.bufs, self.sems = bufs, sems
        self.gather = Gather(self.back)

    def copy(self, src, dst, level, k, b):
        return pltpu.make_async_remote_copy(
            src_ref=src, dst_ref=dst, send_sem=self.sems[2 * level].at[k], recv_sem=self.sems[2 * level + 1].at[k],
            device_id=(self.peers[b],), device_id_type=MESH)

    def swap(self, p, r):
        return self.copy(self.other(p, r), self.bufs[0].at[8 * p + r], 0, 8 * p + r, 0)

    def link(self, p, r, level):
        n = HOPS[level]
        return self.copy(self.own(p, n + r), self.bufs[1 + level].at[n * p + r], 1 + level, n * p + r, 1 + (p + level) % 3)

    def back(self, p, r, level, theirs=False):
        n = HOPS[level]
        if theirs and level == 3:
            dst = self.out.at[self.partner[8 * p + r]]
        else:
            dst = self.out.at[self.mine[8 * p + (r + n if theirs else r)]]
        src = self.own(p, 0) if r == 0 and not theirs else dst
        return self.copy(src, dst, 4 + level, n * p + r, 0 if level == 3 else 1 + (p + level) % 3)

    def keep(self, p):
        return pltpu.make_async_copy(self.own(p, 0), self.out.at[self.mine[8 * p]], self.sems[16].at[p])

    def plus(self, p, r, *terms):
        ref = self.own(p, r)
        value = ref[...]
        for level, k in terms:
            value = value + self.bufs[level][k]
        ref[...] = value

    def start(self):
        for r in reversed(range(8)):
            for p in PARTS:
                if self.load is not None:
                    self.load(p, r).start()
                self.swap(p, r).start()

    def swapped(self, rs):
        for r in rs:
            for p in PARTS:
                if self.load is not None:
                    self.load(p, r).wait()
                self.swap(p, r).wait_recv()
                self.plus(p, r, (0, 8 * p + r))
                if r >= 4:
                    self.link(p, r - 4, 0).start()

    def second(self, r):
        for p in PARTS:
            self.link(p, r, 0).wait_recv()
            self.plus(p, r, (1, 4 * p + r))
            self.link(p, r - 2, 1).start()

    def third(self):
        for p in PARTS:
            self.link(p, 1, 0).wait_recv()
            self.link(p, 1, 1).wait_recv()
            self.plus(p, 1, (1, 4 * p + 1), (2, 2 * p + 1))
            self.link(p, 0, 2).start()

    def finish(self):
        for p in PARTS:
            self.link(p, 0, 0).wait_recv()
            self.link(p, 0, 1).wait_recv()
            self.link(p, 0, 2).wait_recv()
            self.plus(p, 0, (1, 4 * p), (2, 2 * p), (3, p))
        self.gather.begin()
        for p in PARTS:
            self.keep(p).start()

    def close(self):
        self.gather.core(*range(8))
        self.gather.drain()
        for p in PARTS:
            for r in range(8):
                self.swap(p, r).wait_send()
            for level in PARTS:
                for r in range(HOPS[level]):
                    self.link(p, r, level).wait_send()
            self.keep(p).wait()


SUM_BUFS = [pltpu.VMEM((n, PIECE, WIDTH), F32) for n in (24, 12, 6, 3)]
SUM_SEMS = [pltpu.SemaphoreType.DMA((n,)) for n in (24, 12, 6, 3) for _ in range(2)] + HOP_SEMS + [pltpu.SemaphoreType.DMA((3,))]


def gather_kernel(tau_ref, docs_own, x_ref, w1_ref, w2_ref, p_ref, up_ref, stat_ref, q_all, docs, e_ref, m_ref, g_ref, acc, u_ref,
                  q_ref, mine_ref, *sems):
    me = lax.axis_index("data")
    d_sems, q_sems, (share_send, share_recv, local_sem) = sems[:8], sems[8:16], sems[16:]
    inv_tau = 1.0 / tau_ref[0]
    c = inv_tau * LOG2E
    scale = inv_tau / BATCH
    barrier = pltpu.get_barrier_semaphore()
    for p in range(1, ND):
        pl.semaphore_signal(barrier, inc=1, device_id=(lax.rem(me + p, ND),), device_id_type=MESH)
    pl.semaphore_wait(barrier, ND - 1)

    def place(part, r, other=0):
        dev = across(me, 0) if other else me
        for i in range(3):
            if (r >> (2 - i)) & 1:
                dev = dev + (1 - 2 * bit_of(me, 1 + (part + i) % 3)) * (1 << (1 + (part + i) % 3))
        return dev

    def hop(own, everyone, cuts, sem, part, r, level, theirs=False):
        n = HOPS[level]
        ss, rs = sem[2 * level], sem[2 * level + 1]
        rows, lo, hi = own.shape[0], cuts[part], cuts[part + 1]

        def at(dev):
            return pl.ds(pl.multiple_of(dev * rows + lo, 16), hi - lo)

        if theirs:
            src = dst = everyone.at[at(place(part, r, 1) if level == 3 else place(part, r + n))]
        else:
            dst = everyone.at[at(place(part, r))]
            src = own.at[pl.ds(lo, hi - lo)] if r == 0 else dst
        return pltpu.make_async_remote_copy(
            src_ref=src, dst_ref=dst, send_sem=ss.at[n * part + r], recv_sem=rs.at[n * part + r],
            device_id=(across(me, 0 if level == 3 else 1 + (part + level) % 3),), device_id_type=MESH)

    doc = Gather(functools.partial(hop, docs_own, docs, (0, 336, 672, 1024), d_sems))
    qry = Gather(functools.partial(hop, q_ref, q_all, (0, 176, 352, 512), q_sems))
    doc.begin()
    docs[pl.ds(pl.multiple_of(me * CHUNK, CHUNK), CHUNK), :] = docs_own[...]
    m = ROWS // SUB_COUNT

    def forward(i, _):
        at = pl.ds(pl.multiple_of(i * m, m), m)
        h = x_ref[at, :]
        for k in range(2):
            for j in TILES:
                cs = slice(j * COLS, (j + 1) * COLS)
                u_ref[:, cs] = gelu(mm(h, w1_ref[k, :, cs])).astype(BF16)
            h = (h.astype(F32) + mm(u_ref[...], w2_ref[k])).astype(BF16)
        q_ref[at, :] = mm(h, p_ref[...]).astype(BF16)
        return 0

    lax.fori_loop(0, SUB_COUNT, forward, 0)
    local = pltpu.make_async_copy(q_ref, q_all.at[pl.ds(pl.multiple_of(me * ROWS, ROWS), ROWS)], local_sem)
    local.start()
    doc.pass_on(2, 0)
    m_ref[...] = jnp.full_like(m_ref, LOW)
    lane = lax.broadcasted_iota(jnp.int32, (ROWS, 128), 1)

    def device_at(k):
        chip = k // 2
        chip = jnp.where(chip == 3, 4, jnp.where(chip == 4, 3, chip))
        flips = 2 * chip + lax.rem(k, 2)
        return me + sum((1 - 2 * bit_of(me, b)) * (1 << b) * lax.rem(flips // (1 << b), 2) for b in range(4))

    def score(k, carry):
        @pl.when(k == 1)
        def _():
            doc.core(0)

        @pl.when(k == 2)
        def _():
            doc.pass_on(1, 0)
            doc.pass_on(0, 0)

        @pl.when(k == 3)
        def _():
            doc.core(1, 2, 4)

        @pl.when(k == 8)
        def _():
            doc.pass_on(1, 1)
            qry.begin()
            doc.pass_on(0, 1, 2)

        @pl.when(k == 9)
        def _():
            doc.core(3, 5, 6)

        @pl.when(k == 14)
        def _():
            doc.pass_on(0, 3)

        @pl.when(k == 15)
        def _():
            doc.core(7)

        top, total = carry
        base = device_at(k) * CHUNK
        marks = m_ref[...]
        for half in range(2):
            rows = docs[pl.ds(pl.multiple_of(base + half * ROWS, ROWS), ROWS), :]
            s = mm(q_ref[...], rows, LAST)
            best = jnp.max(s, axis=1, keepdims=True)
            e = jnp.exp2((s - best) * c)
            e_ref[k, :, half * ROWS:(half + 1) * ROWS] = e
            marks = jnp.where(lane == 2 * k + half, best, marks)
            new_top = jnp.maximum(top, best)
            total = total * jnp.exp2((top - new_top) * c) + jnp.sum(e, axis=1, keepdims=True) * jnp.exp2((best - new_top) * c)
            top = new_top
        m_ref[...] = marks
        return top, total

    top, total = lax.fori_loop(0, ND, score, (jnp.full((ROWS, 1), LOW, F32), jnp.zeros((ROWS, 1), F32)))
    pos = jnp.sum(q_ref[...].astype(F32) * docs_own[0:ROWS, :].astype(F32), axis=1, keepdims=True)
    loss = (top - pos) * inv_tau + jnp.log(total)
    weight = scale / total
    mine_ref[...] = jnp.where(lane == 0, top, jnp.where(lane == 1, weight, loss)).T[0:8, :]
    stat_ref[me] = mine_ref[...]

    def share(p, slot):
        return pltpu.make_async_remote_copy(
            src_ref=mine_ref, dst_ref=stat_ref.at[slot], send_sem=share_send.at[p], recv_sem=share_recv.at[p],
            device_id=(lax.rem(me + p, ND),), device_id_type=MESH)

    for p in range(1, ND):
        share(p, me).start()
    m_ref[...] = jnp.exp2((m_ref[...] - top) * c) * weight
    qry.pass_on(2, 0)

    def weighted(k, half):
        f = jnp.sum(jnp.where(lane == 2 * k + half, m_ref[...], 0.0), axis=1, keepdims=True)
        return e_ref[k, :, half * ROWS:(half + 1) * ROWS] * f

    r = lax.broadcasted_iota(jnp.int32, (ROWS, ROWS), 0)
    col = lax.broadcasted_iota(jnp.int32, (ROWS, ROWS), 1)
    acc[...] = mm((weighted(0, 0) - jnp.where(r == col, scale, 0.0)).astype(BF16), docs_own[0:ROWS, :])
    acc[...] += mm(weighted(0, 1).astype(BF16), docs_own[ROWS:, :])

    def pull(k, _):
        @pl.when(k == 5)
        def _():
            qry.pass_on(1, 0)
            qry.pass_on(0, 0)

        @pl.when(k == 10)
        def _():
            qry.pass_on(1, 1)

        base = device_at(k) * CHUNK
        for half in range(2):
            g_ref[:, half * ROWS:(half + 1) * ROWS] = weighted(k, half).astype(BF16)
        acc[...] += mm(g_ref[...], docs[pl.ds(pl.multiple_of(base, CHUNK), CHUNK), :])
        return 0

    lax.fori_loop(1, ND, pull, 0)
    up_ref[...] = acc[...].astype(BF16)
    qry.pass_on(0, 1, 2, 3)
    qry.core(*range(8))
    for p in range(1, ND):
        share(p, me).wait_send()
        share(p, lax.rem(me + ND - p, ND)).wait_recv()
    doc.drain()
    qry.drain()
    local.wait()


def gather_rows(tau, docs_own, x, w1, w2, p):
    vmem = pl.BlockSpec(memory_space=pltpu.VMEM)
    return pl.pallas_call(
        gather_kernel,
        out_shape=[
            jax.ShapeDtypeStruct((ROWS, WIDTH), BF16),
            jax.ShapeDtypeStruct((ND, 8, ROWS), F32),
            jax.ShapeDtypeStruct((BATCH, WIDTH), BF16),
        ],
        in_specs=[pl.BlockSpec(memory_space=pltpu.SMEM)] + [vmem] * 5,
        out_specs=[vmem, vmem, pl.BlockSpec(memory_space=pl.ANY)],
        scratch_shapes=[
            pltpu.VMEM((2 * BATCH, WIDTH), BF16),
            pltpu.VMEM((ND, ROWS, CHUNK), F32),
            pltpu.VMEM((ROWS, 128), F32),
            pltpu.VMEM((ROWS, CHUNK), BF16),
            pltpu.VMEM((ROWS, WIDTH), F32),
            pltpu.VMEM((ROWS // SUB_COUNT, FFN), BF16),
            pltpu.VMEM((ROWS, WIDTH), BF16),
            pltpu.VMEM((8, ROWS), F32),
        ] + HOP_SEMS + HOP_SEMS + [pltpu.SemaphoreType.DMA((ND,)), pltpu.SemaphoreType.DMA((ND,)), pltpu.SemaphoreType.DMA],
        compiler_params=pltpu.CompilerParams(collective_id=0, has_side_effects=True, vmem_limit_bytes=VMEM_MAX),
        name="gather_rows",
    )(tau, docs_own, x, w1, w2, p)


def tail_kernel(tau_ref, stat_ref, own_ref, x_ref, w1_ref, w2_ref, p_ref, grads_q, q_ref, out_q, out_d,
                q_buf, g_ref, up_ref, grads, u_ref, s_ref, h_ref, dl_ref, held, q_sem, load_sems, *rest):
    me = lax.axis_index("data")
    inv_tau = 1.0 / tau_ref[0]
    c = inv_tau * LOG2E
    scale = inv_tau / BATCH
    places = mine, partner, peers = sum_places(me)
    barrier = pltpu.get_barrier_semaphore()
    for b in range(4):
        pl.semaphore_signal(barrier, inc=1, device_id=(peers[b],), device_id_type=MESH)
    pl.semaphore_wait(barrier, 4)
    queries = pltpu.make_async_copy(q_ref, q_buf, q_sem)
    queries.start()

    def load(p, r):
        k = 8 * p + r
        return pltpu.make_async_copy(grads_q.at[mine[k]], held.at[k], load_sems.at[k])

    sum_q = DeviceSum(places, lambda p, r: held.at[8 * p + r], lambda p, r: grads_q.at[partner[8 * p + r]], out_q,
                      rest[0:4], rest[8:25], load)
    sum_d = DeviceSum(places, lambda p, r: grads.at[mine[8 * p + r]], lambda p, r: grads.at[partner[8 * p + r]], out_d,
                      rest[4:8], rest[25:42])
    sum_q.start()

    def rows_of(k):
        return pl.ds(pl.multiple_of(lax.rem(me + k, ND) * ROWS, ROWS), ROWS)

    def probs(k):
        j = lax.rem(me + k, ND)
        s = mm(own_ref[...], q_buf[rows_of(k), :], LAST)
        return jnp.exp2((s - stat_ref[j, 0:1, :]) * c) * stat_ref[j, 1:2, :]

    grads[...] = jnp.zeros_like(grads)
    queries.wait()
    row = lax.broadcasted_iota(jnp.int32, (CHUNK, ROWS), 0)
    col = lax.broadcasted_iota(jnp.int32, (CHUNK, ROWS), 1)
    up_ref[...] = mm((probs(0) - jnp.where(row == col, scale, 0.0)).astype(BF16), q_buf[rows_of(0), :])
    sum_q.swapped(FAR)

    def columns(i, _):
        @pl.when(i == 1)
        def _():
            sum_q.swapped(NEAR)

        @pl.when(i == 2)
        def _():
            sum_q.second(3)

        @pl.when(i == 3)
        def _():
            sum_q.second(2)

        for n in range(3):
            k = 3 * i + n + 1
            g_ref[n % 2] = probs(k).astype(BF16)
            up_ref[...] += mm(g_ref[n % 2], q_buf[rows_of(k), :])
        return 0

    lax.fori_loop(0, 5, columns, 0)
    m = CHUNK // SUB_COUNT

    def add(block, value):
        grads[block * WIDTH:(block + 1) * WIDTH, :] += value

    def backward(i, _):
        @pl.when(i == 2)
        def _():
            sum_q.finish()

        @pl.when(i == 3)
        def _():
            sum_q.gather.pass_on(2, 0)

        def middle():
            @pl.when(i == 0)
            def _():
                sum_q.third()

        at = pl.ds(pl.multiple_of(i * m, m), m)
        backward_rows(x_ref[at, :], up_ref[at, :].astype(BF16), w1_ref, w2_ref, p_ref, add, u_ref, s_ref, h_ref, dl_ref, middle)
        return 0

    lax.fori_loop(0, SUB_COUNT, backward, 0)
    sum_d.start()
    sum_q.gather.pass_on(1, 0)
    sum_d.swapped(FAR)
    sum_q.gather.pass_on(1, 1)
    sum_d.swapped(NEAR)
    sum_q.gather.pass_on(0, 0, 1)
    sum_d.second(3)
    sum_q.gather.pass_on(0, 2)
    sum_d.second(2)
    sum_q.gather.pass_on(0, 3)
    sum_d.third()
    sum_d.finish()
    sum_d.gather.pass_on(2, 0)
    sum_d.gather.pass_on(1, 0, 1)
    sum_d.gather.pass_on(0, *range(4))
    sum_q.close()
    sum_d.close()


def tail(tau, stats, own, x, w1, w2, p, grads_q, q_all):
    vmem, hbm = pl.BlockSpec(memory_space=pltpu.VMEM), pl.BlockSpec(memory_space=pl.ANY)
    packed = jax.ShapeDtypeStruct((BLOCKS * WIDTH, WIDTH), F32)
    m = CHUNK // SUB_COUNT
    return pl.pallas_call(
        tail_kernel,
        out_shape=[packed, packed],
        in_specs=[pl.BlockSpec(memory_space=pltpu.SMEM)] + [vmem] * 6 + [hbm, hbm],
        out_specs=[hbm, hbm],
        scratch_shapes=[
            pltpu.VMEM((BATCH, WIDTH), BF16),
            pltpu.VMEM((2, CHUNK, ROWS), BF16),
            pltpu.VMEM((CHUNK, WIDTH), F32),
            pltpu.VMEM((BLOCKS * WIDTH, WIDTH), F32),
            pltpu.VMEM((2, m, FFN), BF16),
            pltpu.VMEM((2, m, FFN), F32),
            pltpu.VMEM((3, m, WIDTH), BF16),
            pltpu.VMEM((m, FFN), BF16),
            pltpu.VMEM((24, PIECE, WIDTH), F32),
            pltpu.SemaphoreType.DMA,
            pltpu.SemaphoreType.DMA((24,)),
        ] + SUM_BUFS + SUM_BUFS + SUM_SEMS + SUM_SEMS,
        compiler_params=pltpu.CompilerParams(collective_id=1, has_side_effects=True, vmem_limit_bytes=VMEM_MAX),
        name="tail",
    )(tau, stats, own, x, w1, w2, p, grads_q, q_all)


def local_step(q_loc, d_loc, temperature, q_w1, q_w2, q_proj, d_w1, d_w2, d_proj):
    tau = temperature.reshape(1)
    d_rows = d_loc.reshape(CHUNK, WIDTH)
    d_reps = tower_forward(d_rows, d_w1, d_w2, d_proj)
    q_up, stats, q_all = gather_rows(tau, d_reps, q_loc, q_w1, q_w2, q_proj)
    loss = jnp.sum(stats[:, 2, :]) / BATCH
    q_grads = tower_backward(q_loc, q_up, q_w1, q_w2, q_proj)
    q_sum, d_sum = tail(tau, stats, d_reps, d_rows, d_w1, d_w2, d_proj, q_grads.reshape(BLOCKS * WIDTH, WIDTH), q_all)
    shapes = [a.shape for a in (q_w1, q_w2, q_proj, d_w1, d_w2, d_proj)]
    packed = (BLOCKS, WIDTH, WIDTH)
    return (loss, *unpack(q_sum.reshape(packed), d_sum.reshape(packed), shapes))


def solution(mesh):
    specs_in = (P("data", None), P(None, "data", None), P(), P(), P(), P(), P(), P(), P())
    specs_out = (P(), P(), P(), P(), P(), P(), P())
    return jax.shard_map(local_step, mesh=mesh, in_specs=specs_in, out_specs=specs_out, check_vma=False)
```

time: 330 us -> 284 us (0.86)
  Pallas kernels: 283 us -> 265 us
  local copies, waits for them, and re-layouts: 28.9 us -> 14 us
  between operations: 16.5 us -> 3.12 us
    pallas_call x2 -> x1, Pallas kernels: 54 us -> 24.1 us  [tower_backward(): pl.pallas_call(backward_kernel, grid=(SUB_COUNT,), out_shape=jax.ShapeDty...]
    slice x3 -> x0, local copies, waits for them, and re-layouts: 15.1 us -> none  [unpack(): return (w1, blocks[8:16].reshape(2, FFN, WIDTH), blocks[16])]
    pallas_call x2, Pallas kernels: 145 us -> 155 us  [the longest x1 144 us: tail(): pl.pallas_call(tail_kernel, out_shape=[packed, packed], in_specs=[pl.Bloc...]
    unnamed x10 -> x14, local copies, waits for them, and re-layouts: 6.29 us -> 14 us
    reshape x2 -> x0, local copies, waits for them, and re-layouts: 5.68 us -> none  [unpack(): blocks[:8].reshape(2, 4, WIDTH, WIDTH).transpose(0, 2, 1, 3)]
  transfers between devices with their start and end apart: 1 -> 0, of which waited for: 0 -> 0; matrix products, arithmetic and copies ran while one was open for 4% -> 0% of each run, Pallas kernels for 53% -> 0%
where the time goes in v2:
time: 284 us; the launch traced here: 283 us
  Pallas kernels  265 us (93%)
  local copies, waits for them, and re-layouts  14 us (5%)
  between operations  3.12 us (1%)
    pallas_call x1, Pallas kernels, tail(): pl.pallas_call(tail_kernel, out_shape=[packed, packed], in_specs=[pl.Bloc...  144 us
    pallas_call x1, Pallas kernels, gather_rows(): pl.pallas_call(gather_kernel, out_shape=[jax.ShapeDtypeStruct((ROWS, WIDT...  76.3 us
    pallas_call x1, Pallas kernels, tower_backward(): pl.pallas_call(backward_kernel, grid=(SUB_COUNT,), out_shape=jax.ShapeDty...  24.1 us
    unnamed x14, local copies, waits for them, and re-layouts  14 us
    pallas_call x1, Pallas kernels, unpack(): pl.pallas_call(unpack_kernel, out_shape=[jax.ShapeDtypeStruct(a, F32) for...  11.5 us
    pallas_call x1, Pallas kernels, tower_forward(): pl.pallas_call(forward_kernel, grid=(SUB_COUNT,), out_shape=jax.ShapeDtyp...  8.7 us

profile of v2, /device:TPU:0, one launch (start us, length us, event | category | flops | bytes accessed | tf_op | source)
XLA Modules:
  0.0 283.3 jit_solution(10750894260292326821)
XLA Ops:
  1.3 0.0 copy-start.2
  1.3 1.7 copy-done.2
  2.9 0.0 copy-start.3
  2.9 1.7 copy-done.3
  4.6 0.0 copy-start.5
  4.6 1.1 copy-done.5
  5.7 0.0 copy-start.6
  5.7 1.0 copy-done.6
  6.7 8.7 %tower_forward.1.docs_own.own_ref = bf16[1024,384]{1,0:T(8,128)(2,1)S(1)} custom-call(bf16[1024,384]{1,0:T(8,128)(2,1)S(1)} %bitcast.10, bf16[2,384,1536]{2,1,0:T(8,128)(2,1)S(1)} %copy-done.2, bf16[2,1536,384]{2,1,0:T(8,128)(2,1)S(1)} %copy-done.3, bf16[384,384]{1,0:T(8,128)(2,1)S(1)} %copy-done.6), custom_call_target="tpu_custom_call" | custom-call | tf_op jit(solution)/shard_map/tower_forward/pallas_call | solution.py:69
  15.4 0.0 copy-start.4
  15.4 0.9 copy-done.4
  16.3 76.3 %gather_rows.1 = (bf16[512,384]{1,0:T(8,128)(2,1)}, f32[16,8,512]{2,1,0:T(8,128)}, bf16[8192,384]{1,0:T(8,128)(2,1)}) custom-call(f32[1]{0:T(128)} %bitcast.5.tau_ref, bf16[1024,384]{1,0:T(8,128)(2,1)} %copy-done.4, bf16[512,384]{1,0:T(8,128)(2,1)} %x_ref.3, bf16[2,384,1536]{2,1,0:T(8,128)(2,1)} %w1_ref.6, bf16[2,1536,384]{2,1,0:T(8,128)(2,1)} %w2_ref.6, ...), custom_call_target="tpu_custom_call" | custom-call | tf_op jit(solution)/shard_map/gather_rows/pallas_call | solution.py:502
  92.6 1.6 slice_reduce_fusion
  94.8 24.1 %tower_backward.1 = f32[17,384,384]{2,1,0:T(8,128)} custom-call(bf16[512,384]{1,0:T(8,128)(2,1)} %x_ref.3, bf16[512,384]{1,0:T(8,128)(2,1)} %get-tuple-element.19.g_ref, bf16[2,384,1536]{2,1,0:T(8,128)(2,1)} %w1_ref.6, bf16[2,1536,384]{2,1,0:T(8,128)(2,1)} %w2_ref.6, bf16[384,384]{1,0:T(8,128)(2,1)} %p_ref.6), custom_call_target="tpu_custom_call" | custom-call | tf_op jit(solution)/shard_map/tower_backward/pallas_call | solution.py:126
  119.0 144.0 %tail.1 = (f32[6528,384]{1,0:T(8,128)}, f32[6528,384]{1,0:T(8,128)}) custom-call(f32[1]{0:T(128)} %bitcast.6.tau_ref, f32[16,8,512]{2,1,0:T(8,128)} %get-tuple-element.18.stat_ref, bf16[1024,384]{1,0:T(8,128)(2,1)} %copy-done.4, bf16[1024,384]{1,0:T(8,128)(2,1)} %bitcast.9, bf16[2,384,1536]{2,1,0:T(8,128)(2,1)} %w1_ref.7, bf16[2,1536,384]{2,1,0:T(8,128)(2,1)} %w2_ref.7, ...), custom_call_target="tpu_custom_call" | custom-call | tf_op jit(solution)/shard_map/tail/pallas_call | solution.py:632
  263.0 0.0 copy-start
  263.0 3.8 %copy-done = f32[6528,384]{1,0:T(8,128)S(1)} copy-done((f32[6528,384]{1,0:T(8,128)S(1)}, f32[6528,384]{1,0:T(8,128)}, u32[]{:S(2)}) %copy-start) | copy-done | bytes 10027032
  266.8 0.0 copy-start.1
  266.8 3.8 %copy-done.1 = f32[6528,384]{1,0:T(8,128)S(1)} copy-done((f32[6528,384]{1,0:T(8,128)S(1)}, f32[6528,384]{1,0:T(8,128)}, u32[]{:S(2)}) %copy-start.1) | copy-done | bytes 10027032
  270.7 11.5 %unpack.1 = (f32[2,384,1536]{2,1,0:T(8,128)}, f32[2,1536,384]{2,1,0:T(8,128)}, f32[384,384]{1,0:T(8,128)}, f32[2,384,1536]{2,1,0:T(8,128)}, f32[2,1536,384]{2,1,0:T(8,128)}, /*index=5*/f32[384,384]{1,0:T(8,128)}) custom-call(f32[17,384,384]{2,1,0:T(8,128)S(1)} %bitcast.7, f32[17,384,384]{2,1,0:T(8,128)S(1)} %bitcast.8), custom_call_target="tpu_custom_call" | custom-call | tf_op jit(solution)/shard_map/unpack/pallas_call | solution.py:172
Async XLA Ops:
  1.3 1.7 copy-start.2
  2.9 1.7 copy-start.3
  4.6 1.1 copy-start.5
  5.7 1.0 copy-start.6
  15.4 0.9 copy-start.4
  263.0 3.8 %copy-start = (f32[6528,384]{1,0:T(8,128)S(1)}, f32[6528,384]{1,0:T(8,128)}, u32[]{:S(2)}) copy-start(f32[6528,384]{1,0:T(8,128)} %get-tuple-element.21) | copy-start | bytes 30081028
  266.8 3.8 %copy-start.1 = (f32[6528,384]{1,0:T(8,128)S(1)}, f32[6528,384]{1,0:T(8,128)}, u32[]{:S(2)}) copy-start(f32[6528,384]{1,0:T(8,128)} %get-tuple-element.22) | copy-start | bytes 30081028

commit v3 on v2

--- a/solution.py
+++ b/solution.py
@@ -52,28 +52,51 @@
     return a * cdf, slope
 
 
-def forward_kernel(x_ref, w1_ref, w2_ref, p_ref, y_ref, u_ref):
-    h = x_ref[...]
-    for k in range(2):
-        for c in TILES:
-            cs = slice(c * COLS, (c + 1) * COLS)
-            u_ref[:, cs] = gelu(mm(h, w1_ref[k, :, cs])).astype(BF16)
-        h = (h.astype(F32) + mm(u_ref[...], w2_ref[k])).astype(BF16)
-    y_ref[...] = mm(h, p_ref[...]).astype(BF16)
+def fetches(srcs, dsts, sems):
+    return [pltpu.make_async_copy(src, dst, sems.at[i]) for i, (src, dst) in enumerate(zip(srcs, dsts))]
+
+
+def forward_rows(x_ref, y_ref, w1_ref, w2_ref, p_ref, u_ref):
+    m = x_ref.shape[0] // SUB_COUNT
+
+    def step(i, _):
+        at = pl.ds(pl.multiple_of(i * m, m), m)
+        h = x_ref[at, :]
+        for k in range(2):
+            for j in TILES:
+                cs = slice(j * COLS, (j + 1) * COLS)
+                u_ref[:, cs] = gelu(mm(h, w1_ref[k, :, cs])).astype(BF16)
+            h = (h.astype(F32) + mm(u_ref[...], w2_ref[k])).astype(BF16)
+        y_ref[at, :] = mm(h, p_ref[...]).astype(BF16)
+        return 0
+
+    lax.fori_loop(0, SUB_COUNT, step, 0)
+
+
+WEIGHTS = [
+    pltpu.VMEM((2, WIDTH, FFN), BF16), pltpu.VMEM((2, FFN, WIDTH), BF16), pltpu.VMEM((WIDTH, WIDTH), BF16),
+    pltpu.SemaphoreType.DMA((3,))]
+INNER, OUTER = pl.BlockSpec(memory_space=pltpu.VMEM), pl.BlockSpec(memory_space=pltpu.HBM)
+SCALAR = pl.BlockSpec(memory_space=pltpu.SMEM)
+
+
+def forward_kernel(x_ref, w1_ref, w2_ref, p_ref, y_ref, u_ref, w1, w2, p, w_sems):
+    loads = fetches((w1_ref, w2_ref, p_ref), (w1, w2, p), w_sems)
+    for load in loads:
+        load.start()
+    for load in loads:
+        load.wait()
+    forward_rows(x_ref, y_ref, w1, w2, p, u_ref)
 
 
 def tower_forward(rows, w1, w2, p):
-    n = rows.shape[0]
-    m = n // SUB_COUNT
-    whole = lambda a: pl.BlockSpec(a.shape, lambda i: (0,) * a.ndim)
     return pl.pallas_call(
         forward_kernel,
-        grid=(SUB_COUNT,),
-        out_shape=jax.ShapeDtypeStruct((n, WIDTH), BF16),
-        in_specs=[pl.BlockSpec((m, WIDTH), lambda i: (i, 0)), whole(w1), whole(w2), whole(p)],
-        out_specs=pl.BlockSpec((m, WIDTH), lambda i: (i, 0)),
-        scratch_shapes=[pltpu.VMEM((m, FFN), BF16)],
-        compiler_params=pltpu.CompilerParams(vmem_limit_bytes=40 << 20),
+        out_shape=jax.ShapeDtypeStruct(rows.shape, BF16),
+        in_specs=[INNER] + [OUTER] * 3,
+        out_specs=INNER,
+        scratch_shapes=[pltpu.VMEM((rows.shape[0] // SUB_COUNT, FFN), BF16)] + WEIGHTS,
+        compiler_params=pltpu.CompilerParams(vmem_limit_bytes=VMEM_MAX),
         name="tower_forward",
     )(rows, w1, w2, p)
 
@@ -107,39 +130,6 @@
             e = e + mm(dl_ref[...], w1_ref[k], LAST)
 
 
-def backward_kernel(x_ref, g_ref, w1_ref, w2_ref, p_ref, out_ref, u_ref, s_ref, h_ref, dl_ref):
-    @pl.when(pl.program_id(0) == 0)
-    def _():
-        out_ref[...] = jnp.zeros_like(out_ref)
-
-    def add(block, value):
-        out_ref[block] += value
-
-    backward_rows(x_ref[...], g_ref[...], w1_ref, w2_ref, p_ref, add, u_ref, s_ref, h_ref, dl_ref)
-
-
-def tower_backward(rows, up, w1, w2, p):
-    n = rows.shape[0]
-    m = n // SUB_COUNT
-    whole = lambda a: pl.BlockSpec(a.shape, lambda i: (0,) * a.ndim)
-    block = pl.BlockSpec((m, WIDTH), lambda i: (i, 0))
-    return pl.pallas_call(
-        backward_kernel,
-        grid=(SUB_COUNT,),
-        out_shape=jax.ShapeDtypeStruct((BLOCKS, WIDTH, WIDTH), F32),
-        in_specs=[block, block, whole(w1), whole(w2), whole(p)],
-        out_specs=pl.BlockSpec((BLOCKS, WIDTH, WIDTH), lambda i: (0, 0, 0)),
-        scratch_shapes=[
-            pltpu.VMEM((2, m, FFN), BF16),
-            pltpu.VMEM((2, m, FFN), F32),
-            pltpu.VMEM((3, m, WIDTH), BF16),
-            pltpu.VMEM((m, FFN), BF16),
-        ],
-        compiler_params=pltpu.CompilerParams(vmem_limit_bytes=60 << 20),
-        name="tower_backward",
-    )(rows, up, w1, w2, p)
-
-
 def unpack_kernel(q_ref, d_ref, *refs):
     outs, hold, load, store = refs[:6], refs[6], refs[7], refs[8]
 
@@ -168,12 +158,11 @@
 
 
 def unpack(q_blocks, d_blocks, shapes):
-    hbm = pl.BlockSpec(memory_space=pl.ANY)
     return pl.pallas_call(
         unpack_kernel,
         out_shape=[jax.ShapeDtypeStruct(a, F32) for a in shapes],
-        in_specs=[hbm, hbm],
-        out_specs=[hbm] * 6,
+        in_specs=[OUTER, OUTER],
+        out_specs=[OUTER] * 6,
         scratch_shapes=[
             pltpu.VMEM((2 * BLOCKS, WIDTH, WIDTH), F32),
             pltpu.SemaphoreType.DMA((2 * BLOCKS,)),
@@ -232,6 +221,32 @@
                     self.copy(p, r, level).wait_send()
 
 
+def place(me, part, r, other=0):
+    dev = across(me, 0) if other else me
+    for i in range(3):
+        if (r >> (2 - i)) & 1:
+            dev = dev + (1 - 2 * bit_of(me, 1 + (part + i) % 3)) * (1 << (1 + (part + i) % 3))
+    return dev
+
+
+def hop(me, own, everyone, cuts, sem, part, r, level, theirs=False):
+    n = HOPS[level]
+    ss, rs = sem[2 * level], sem[2 * level + 1]
+    rows, lo, hi = own.shape[0], cuts[part], cuts[part + 1]
+
+    def at(dev):
+        return pl.ds(pl.multiple_of(dev * rows + lo, 16), hi - lo)
+
+    if theirs:
+        src = dst = everyone.at[at(place(me, part, r, 1) if level == 3 else place(me, part, r + n))]
+    else:
+        dst = everyone.at[at(place(me, part, r))]
+        src = own.at[pl.ds(lo, hi - lo)] if r == 0 else dst
+    return pltpu.make_async_remote_copy(
+        src_ref=src, dst_ref=dst, send_sem=ss.at[n * part + r], recv_sem=rs.at[n * part + r],
+        device_id=(across(me, 0 if level == 3 else 1 + (part + level) % 3),), device_id_type=MESH)
+
+
 HOP_SEMS = [pltpu.SemaphoreType.DMA((3 * n,)) for n in HOPS for _ in range(2)]
 
 
@@ -329,10 +344,12 @@
 SUM_SEMS = [pltpu.SemaphoreType.DMA((n,)) for n in (24, 12, 6, 3) for _ in range(2)] + HOP_SEMS + [pltpu.SemaphoreType.DMA((3,))]
 
 
-def gather_kernel(tau_ref, docs_own, x_ref, w1_ref, w2_ref, p_ref, up_ref, stat_ref, q_all, docs, e_ref, m_ref, g_ref, acc, u_ref,
-                  q_ref, mine_ref, *sems):
+def gather_kernel(tau_ref, docs_own, x_ref, w1_ref, w2_ref, p_ref, up_ref, stat_ref, q_ref, docs, e_ref, m_ref, g_ref, acc, u_ref,
+                  mine_ref, w1, w2, p_w, w_sems, share_send, share_recv, *d_sems):
     me = lax.axis_index("data")
-    d_sems, q_sems, (share_send, share_recv, local_sem) = sems[:8], sems[8:16], sems[16:]
+    loads = fetches((w1_ref, w2_ref, p_ref), (w1, w2, p_w), w_sems)
+    for load in loads:
+        load.start()
     inv_tau = 1.0 / tau_ref[0]
     c = inv_tau * LOG2E
     scale = inv_tau / BATCH
@@ -341,50 +358,12 @@
         pl.semaphore_signal(barrier, inc=1, device_id=(lax.rem(me + p, ND),), device_id_type=MESH)
     pl.semaphore_wait(barrier, ND - 1)
 
-    def place(part, r, other=0):
-        dev = across(me, 0) if other else me
-        for i in range(3):
-            if (r >> (2 - i)) & 1:
-                dev = dev + (1 - 2 * bit_of(me, 1 + (part + i) % 3)) * (1 << (1 + (part + i) % 3))
-        return dev
-
-    def hop(own, everyone, cuts, sem, part, r, level, theirs=False):
-        n = HOPS[level]
-        ss, rs = sem[2 * level], sem[2 * level + 1]
-        rows, lo, hi = own.shape[0], cuts[part], cuts[part + 1]
-
-        def at(dev):
-            return pl.ds(pl.multiple_of(dev * rows + lo, 16), hi - lo)
-
-        if theirs:
-            src = dst = everyone.at[at(place(part, r, 1) if level == 3 else place(part, r + n))]
-        else:
-            dst = everyone.at[at(place(part, r))]
-            src = own.at[pl.ds(lo, hi - lo)] if r == 0 else dst
-        return pltpu.make_async_remote_copy(
-            src_ref=src, dst_ref=dst, send_sem=ss.at[n * part + r], recv_sem=rs.at[n * part + r],
-            device_id=(across(me, 0 if level == 3 else 1 + (part + level) % 3),), device_id_type=MESH)
-
-    doc = Gather(functools.partial(hop, docs_own, docs, (0, 336, 672, 1024), d_sems))
-    qry = Gather(functools.partial(hop, q_ref, q_all, (0, 176, 352, 512), q_sems))
+    doc = Gather(functools.partial(hop, me, docs_own, docs, (0, 336, 672, 1024), d_sems))
     doc.begin()
     docs[pl.ds(pl.multiple_of(me * CHUNK, CHUNK), CHUNK), :] = docs_own[...]
-    m = ROWS // SUB_COUNT
-
-    def forward(i, _):
-        at = pl.ds(pl.multiple_of(i * m, m), m)
-        h = x_ref[at, :]
-        for k in range(2):
-            for j in TILES:
-                cs = slice(j * COLS, (j + 1) * COLS)
-                u_ref[:, cs] = gelu(mm(h, w1_ref[k, :, cs])).astype(BF16)
-            h = (h.astype(F32) + mm(u_ref[...], w2_ref[k])).astype(BF16)
-        q_ref[at, :] = mm(h, p_ref[...]).astype(BF16)
-        return 0
-
-    lax.fori_loop(0, SUB_COUNT, forward, 0)
-    local = pltpu.make_async_copy(q_ref, q_all.at[pl.ds(pl.multiple_of(me * ROWS, ROWS), ROWS)], local_sem)
-    local.start()
+    for load in loads:
+        load.wait()
+    forward_rows(x_ref, q_ref, w1, w2, p_w, u_ref)
     doc.pass_on(2, 0)
     m_ref[...] = jnp.full_like(m_ref, LOW)
     lane = lax.broadcasted_iota(jnp.int32, (ROWS, 128), 1)
@@ -412,7 +391,6 @@
         @pl.when(k == 8)
         def _():
             doc.pass_on(1, 1)
-            qry.begin()
             doc.pass_on(0, 1, 2)
 
         @pl.when(k == 9)
@@ -458,7 +436,6 @@
     for p in range(1, ND):
         share(p, me).start()
     m_ref[...] = jnp.exp2((m_ref[...] - top) * c) * weight
-    qry.pass_on(2, 0)
 
     def weighted(k, half):
         f = jnp.sum(jnp.where(lane == 2 * k + half, m_ref[...], 0.0), axis=1, keepdims=True)
@@ -470,15 +447,6 @@
     acc[...] += mm(weighted(0, 1).astype(BF16), docs_own[ROWS:, :])
 
     def pull(k, _):
-        @pl.when(k == 5)
-        def _():
-            qry.pass_on(1, 0)
-            qry.pass_on(0, 0)
-
-        @pl.when(k == 10)
-        def _():
-            qry.pass_on(1, 1)
-
         base = device_at(k) * CHUNK
         for half in range(2):
             g_ref[:, half * ROWS:(half + 1) * ROWS] = weighted(k, half).astype(BF16)
@@ -487,27 +455,19 @@
 
     lax.fori_loop(1, ND, pull, 0)
     up_ref[...] = acc[...].astype(BF16)
-    qry.pass_on(0, 1, 2, 3)
-    qry.core(*range(8))
     for p in range(1, ND):
         share(p, me).wait_send()
         share(p, lax.rem(me + ND - p, ND)).wait_recv()
     doc.drain()
-    qry.drain()
-    local.wait()
 
 
 def gather_rows(tau, docs_own, x, w1, w2, p):
-    vmem = pl.BlockSpec(memory_space=pltpu.VMEM)
+    mine = jax.ShapeDtypeStruct((ROWS, WIDTH), BF16)
     return pl.pallas_call(
         gather_kernel,
-        out_shape=[
-            jax.ShapeDtypeStruct((ROWS, WIDTH), BF16),
-            jax.ShapeDtypeStruct((ND, 8, ROWS), F32),
-            jax.ShapeDtypeStruct((BATCH, WIDTH), BF16),
-        ],
-        in_specs=[pl.BlockSpec(memory_space=pltpu.SMEM)] + [vmem] * 5,
-        out_specs=[vmem, vmem, pl.BlockSpec(memory_space=pl.ANY)],
+        out_shape=[mine, jax.ShapeDtypeStruct((ND, 8, ROWS), F32), mine],
+        in_specs=[SCALAR, INNER, INNER] + [OUTER] * 3,
+        out_specs=[INNER] * 3,
         scratch_shapes=[
             pltpu.VMEM((2 * BATCH, WIDTH), BF16),
             pltpu.VMEM((ND, ROWS, CHUNK), F32),
@@ -515,25 +475,92 @@
             pltpu.VMEM((ROWS, CHUNK), BF16),
             pltpu.VMEM((ROWS, WIDTH), F32),
             pltpu.VMEM((ROWS // SUB_COUNT, FFN), BF16),
-            pltpu.VMEM((ROWS, WIDTH), BF16),
             pltpu.VMEM((8, ROWS), F32),
-        ] + HOP_SEMS + HOP_SEMS + [pltpu.SemaphoreType.DMA((ND,)), pltpu.SemaphoreType.DMA((ND,)), pltpu.SemaphoreType.DMA],
+        ] + WEIGHTS + [pltpu.SemaphoreType.DMA((ND,)), pltpu.SemaphoreType.DMA((ND,))] + HOP_SEMS,
         compiler_params=pltpu.CompilerParams(collective_id=0, has_side_effects=True, vmem_limit_bytes=VMEM_MAX),
         name="gather_rows",
     )(tau, docs_own, x, w1, w2, p)
 
 
+def greet(peers):
+    barrier = pltpu.get_barrier_semaphore()
+    for peer in peers:
+        pl.semaphore_signal(barrier, inc=1, device_id=(peer,), device_id_type=MESH)
+    pl.semaphore_wait(barrier, len(peers))
+
+
+def query_kernel(q_ref, x_ref, up_ref, w1_ref, w2_ref, p_ref, out_ref, q_all, u_ref, s_ref, h_ref, dl_ref, w1, w2, p, w_sems,
+                 local_sem, *sems):
+    me = lax.axis_index("data")
+    loads = fetches((w1_ref, w2_ref, p_ref), (w1, w2, p), w_sems)
+    for load in loads:
+        load.start()
+    greet([across(me, b) for b in range(4)])
+    qry = Gather(functools.partial(hop, me, q_ref, q_all, (0, 176, 352, 512), sems))
+    qry.begin()
+    local = pltpu.make_async_copy(q_ref, q_all.at[pl.ds(pl.multiple_of(me * ROWS, ROWS), ROWS)], local_sem)
+    local.start()
+    out_ref[...] = jnp.zeros_like(out_ref)
+    for load in loads:
+        load.wait()
+    m = ROWS // SUB_COUNT
+
+    def add(block, value):
+        out_ref[block * WIDTH:(block + 1) * WIDTH, :] += value
+
+    def step(i, _):
+        @pl.when(i == 1)
+        def _():
+            qry.pass_on(2, 0)
+
+        @pl.when(i == 2)
+        def _():
+            qry.pass_on(1, 0)
+            qry.pass_on(0, 0)
+
+        @pl.when(i == 3)
+        def _():
+            qry.pass_on(1, 1)
+
+        at = pl.ds(pl.multiple_of(i * m, m), m)
+        backward_rows(x_ref[at, :], up_ref[at, :], w1, w2, p, add, u_ref, s_ref, h_ref, dl_ref)
+        return 0
+
+    lax.fori_loop(0, SUB_COUNT, step, 0)
+    qry.pass_on(0, 1, 2, 3)
+    qry.core(*range(8))
+    qry.drain()
+    local.wait()
+
+
+def backward_scratch(m):
+    return [pltpu.VMEM((2, m, FFN), BF16), pltpu.VMEM((2, m, FFN), F32), pltpu.VMEM((3, m, WIDTH), BF16), pltpu.VMEM((m, FFN), BF16)]
+
+
+PACKED = jax.ShapeDtypeStruct((BLOCKS * WIDTH, WIDTH), F32)
+
+
+def query_backward(q, x, up, w1, w2, p):
+    return pl.pallas_call(
+        query_kernel,
+        out_shape=[PACKED, jax.ShapeDtypeStruct((BATCH, WIDTH), BF16)],
+        in_specs=[INNER] * 3 + [OUTER] * 3,
+        out_specs=[INNER, OUTER],
+        scratch_shapes=backward_scratch(ROWS // SUB_COUNT) + WEIGHTS + [pltpu.SemaphoreType.DMA] + HOP_SEMS,
+        compiler_params=pltpu.CompilerParams(collective_id=2, has_side_effects=True, vmem_limit_bytes=VMEM_MAX),
+        name="query_backward",
+    )(q, x, up, w1, w2, p)
+
+
 def tail_kernel(tau_ref, stat_ref, own_ref, x_ref, w1_ref, w2_ref, p_ref, grads_q, q_ref, out_q, out_d,
-                q_buf, g_ref, up_ref, grads, u_ref, s_ref, h_ref, dl_ref, held, q_sem, load_sems, *rest):
+                q_buf, g_ref, up_ref, grads, u_ref, s_ref, h_ref, dl_ref, w1, w2, p_w, w_sems, held, q_sem, load_sems, *rest):
     me = lax.axis_index("data")
+    loads = fetches((w1_ref, w2_ref, p_ref), (w1, w2, p_w), w_sems)
     inv_tau = 1.0 / tau_ref[0]
     c = inv_tau * LOG2E
     scale = inv_tau / BATCH
     places = mine, partner, peers = sum_places(me)
-    barrier = pltpu.get_barrier_semaphore()
-    for b in range(4):
-        pl.semaphore_signal(barrier, inc=1, device_id=(peers[b],), device_id_type=MESH)
-    pl.semaphore_wait(barrier, 4)
+    greet(peers)
     queries = pltpu.make_async_copy(q_ref, q_buf, q_sem)
     queries.start()
 
@@ -546,6 +573,8 @@
     sum_d = DeviceSum(places, lambda p, r: grads.at[mine[8 * p + r]], lambda p, r: grads.at[partner[8 * p + r]], out_d,
                       rest[4:8], rest[25:42])
     sum_q.start()
+    for load in loads:
+        load.start()
 
     def rows_of(k):
         return pl.ds(pl.multiple_of(lax.rem(me + k, ND) * ROWS, ROWS), ROWS)
@@ -582,6 +611,8 @@
         return 0
 
     lax.fori_loop(0, 5, columns, 0)
+    for load in loads:
+        load.wait()
     m = CHUNK // SUB_COUNT
 
     def add(block, value):
@@ -602,7 +633,7 @@
                 sum_q.third()
 
         at = pl.ds(pl.multiple_of(i * m, m), m)
-        backward_rows(x_ref[at, :], up_ref[at, :].astype(BF16), w1_ref, w2_ref, p_ref, add, u_ref, s_ref, h_ref, dl_ref, middle)
+        backward_rows(x_ref[at, :], up_ref[at, :].astype(BF16), w1, w2, p_w, add, u_ref, s_ref, h_ref, dl_ref, middle)
         return 0
 
     lax.fori_loop(0, SUB_COUNT, backward, 0)
@@ -626,23 +657,17 @@
 
 
 def tail(tau, stats, own, x, w1, w2, p, grads_q, q_all):
-    vmem, hbm = pl.BlockSpec(memory_space=pltpu.VMEM), pl.BlockSpec(memory_space=pl.ANY)
-    packed = jax.ShapeDtypeStruct((BLOCKS * WIDTH, WIDTH), F32)
-    m = CHUNK // SUB_COUNT
     return pl.pallas_call(
         tail_kernel,
-        out_shape=[packed, packed],
-        in_specs=[pl.BlockSpec(memory_space=pltpu.SMEM)] + [vmem] * 6 + [hbm, hbm],
-        out_specs=[hbm, hbm],
+        out_shape=[PACKED, PACKED],
+        in_specs=[SCALAR] + [INNER] * 3 + [OUTER] * 5,
+        out_specs=[OUTER, OUTER],
         scratch_shapes=[
             pltpu.VMEM((BATCH, WIDTH), BF16),
             pltpu.VMEM((2, CHUNK, ROWS), BF16),
             pltpu.VMEM((CHUNK, WIDTH), F32),
-            pltpu.VMEM((BLOCKS * WIDTH, WIDTH), F32),
-            pltpu.VMEM((2, m, FFN), BF16),
-            pltpu.VMEM((2, m, FFN), F32),
-            pltpu.VMEM((3, m, WIDTH), BF16),
-            pltpu.VMEM((m, FFN), BF16),
+            pltpu.VMEM(PACKED.shape, F32),
+        ] + backward_scratch(CHUNK // SUB_COUNT) + WEIGHTS + [
             pltpu.VMEM((24, PIECE, WIDTH), F32),
             pltpu.SemaphoreType.DMA,
             pltpu.SemaphoreType.DMA((24,)),
@@ -656,10 +681,10 @@
     tau = temperature.reshape(1)
     d_rows = d_loc.reshape(CHUNK, WIDTH)
     d_reps = tower_forward(d_rows, d_w1, d_w2, d_proj)
-    q_up, stats, q_all = gather_rows(tau, d_reps, q_loc, q_w1, q_w2, q_proj)
+    q_up, stats, q_reps = gather_rows(tau, d_reps, q_loc, q_w1, q_w2, q_proj)
     loss = jnp.sum(stats[:, 2, :]) / BATCH
-    q_grads = tower_backward(q_loc, q_up, q_w1, q_w2, q_proj)
-    q_sum, d_sum = tail(tau, stats, d_reps, d_rows, d_w1, d_w2, d_proj, q_grads.reshape(BLOCKS * WIDTH, WIDTH), q_all)
+    q_grads, q_all = query_backward(q_reps, q_loc, q_up, q_w1, q_w2, q_proj)
+    q_sum, d_sum = tail(tau, stats, d_reps, d_rows, d_w1, d_w2, d_proj, q_grads, q_all)
     shapes = [a.shape for a in (q_w1, q_w2, q_proj, d_w1, d_w2, d_proj)]
     packed = (BLOCKS, WIDTH, WIDTH)
     return (loss, *unpack(q_sum.reshape(packed), d_sum.reshape(packed), shapes))

time: 284 us -> 278 us (0.979)
  local copies, waits for them, and re-layouts: 14 us -> 7.69 us
    unnamed x14 -> x4, local copies, waits for them, and re-layouts: 14 us -> 7.69 us
where the time goes in v3:
time: 278 us; the launch traced here: 277 us
  Pallas kernels  265 us (95%)
  local copies, waits for them, and re-layouts  7.69 us (3%)
  between operations  3.11 us (1%)
    pallas_call x1, Pallas kernels, tail(): pl.pallas_call(tail_kernel, out_shape=[PACKED, PACKED], in_specs=[SCALAR]...  142 us
    pallas_call x1, Pallas kernels, gather_rows(): pl.pallas_call(gather_kernel, out_shape=[mine, jax.ShapeDtypeStruct((ND,...  68.1 us
    pallas_call x1, Pallas kernels, query_backward(): pl.pallas_call(query_kernel, out_shape=[PACKED, jax.ShapeDtypeStruct((BAT...  30.4 us
    pallas_call x1, Pallas kernels, tower_forward(): pl.pallas_call(forward_kernel, out_shape=jax.ShapeDtypeStruct(rows.shape,...  13.1 us
    pallas_call x1, Pallas kernels, unpack(): pl.pallas_call(unpack_kernel, out_shape=[jax.ShapeDtypeStruct(a, F32) for...  11.5 us
    unnamed x4, local copies, waits for them, and re-layouts  7.69 us

profile of v3, /device:TPU:0, one launch (start us, length us, event | category | flops | bytes accessed | tf_op | source)
XLA Modules:
  0.0 277.5 jit_solution(6311843059618575195)
XLA Ops:
  1.3 13.1 %tower_forward.1.docs_own.own_ref = bf16[1024,384]{1,0:T(8,128)(2,1)} custom-call(bf16[1024,384]{1,0:T(8,128)(2,1)} %bitcast.8, bf16[2,384,1536]{2,1,0:T(8,128)(2,1)} %w1_ref.7, bf16[2,1536,384]{2,1,0:T(8,128)(2,1)} %w2_ref.7, bf16[384,384]{1,0:T(8,128)(2,1)} %p_ref.7), custom_call_target="tpu_custom_call" | custom-call | tf_op jit(solution)/shard_map/tower_forward/pallas_call | solution.py:93
  14.4 68.1 %gather_rows.1 = (bf16[512,384]{1,0:T(8,128)(2,1)}, f32[16,8,512]{2,1,0:T(8,128)}, bf16[512,384]{1,0:T(8,128)(2,1)}) custom-call(f32[1]{0:T(128)} %bitcast.4.tau_ref, bf16[1024,384]{1,0:T(8,128)(2,1)} %tower_forward.1.docs_own.own_ref, bf16[512,384]{1,0:T(8,128)(2,1)} %x_ref.3, bf16[2,384,1536]{2,1,0:T(8,128)(2,1)} %w1_ref.6, bf16[2,1536,384]{2,1,0:T(8,128)(2,1)} %w2_ref.6, ...), custom_call_target="tpu_custom_call" | custom-call | tf_op jit(solution)/shard_map/gather_rows/pallas_call | solution.py:466
  82.5 1.6 slice_reduce_fusion
  84.8 30.4 %query_backward.1 = (f32[6528,384]{1,0:T(8,128)}, bf16[8192,384]{1,0:T(8,128)(2,1)}) custom-call(bf16[512,384]{1,0:T(8,128)(2,1)} %get-tuple-element.21.q_ref, bf16[512,384]{1,0:T(8,128)(2,1)} %x_ref.3, bf16[512,384]{1,0:T(8,128)(2,1)} %get-tuple-element.22.up_ref, bf16[2,384,1536]{2,1,0:T(8,128)(2,1)} %w1_ref.6, bf16[2,1536,384]{2,1,0:T(8,128)(2,1)} %w2_ref.6, ...), custom_call_target="tpu_custom_call" | custom-call | tf_op jit(solution)/shard_map/query_backward/pallas_call | solution.py:544
  115.2 142.0 %tail.1 = (f32[6528,384]{1,0:T(8,128)}, f32[6528,384]{1,0:T(8,128)}) custom-call(f32[1]{0:T(128)} %bitcast.5.tau_ref, f32[16,8,512]{2,1,0:T(8,128)} %get-tuple-element.20.stat_ref, bf16[1024,384]{1,0:T(8,128)(2,1)} %tower_forward.1.docs_own.own_ref, bf16[1024,384]{1,0:T(8,128)(2,1)} %bitcast.9, bf16[2,384,1536]{2,1,0:T(8,128)(2,1)} %w1_ref.7, ...), custom_call_target="tpu_custom_call" | custom-call | tf_op jit(solution)/shard_map/tail/pallas_call | solution.py:660
  257.2 0.0 copy-start
  257.2 3.8 %copy-done = f32[6528,384]{1,0:T(8,128)S(1)} copy-done((f32[6528,384]{1,0:T(8,128)S(1)}, f32[6528,384]{1,0:T(8,128)}, u32[]{:S(2)}) %copy-start) | copy-done | bytes 10027032
  261.0 0.0 copy-start.1
  261.0 3.8 %copy-done.1 = f32[6528,384]{1,0:T(8,128)S(1)} copy-done((f32[6528,384]{1,0:T(8,128)S(1)}, f32[6528,384]{1,0:T(8,128)}, u32[]{:S(2)}) %copy-start.1) | copy-done | bytes 10027032
  264.9 11.5 %unpack.1 = (f32[2,384,1536]{2,1,0:T(8,128)}, f32[2,1536,384]{2,1,0:T(8,128)}, f32[384,384]{1,0:T(8,128)}, f32[2,384,1536]{2,1,0:T(8,128)}, f32[2,1536,384]{2,1,0:T(8,128)}, /*index=5*/f32[384,384]{1,0:T(8,128)}) custom-call(f32[17,384,384]{2,1,0:T(8,128)S(1)} %bitcast.6, f32[17,384,384]{2,1,0:T(8,128)S(1)} %bitcast.7), custom_call_target="tpu_custom_call" | custom-call | tf_op jit(solution)/shard_map/unpack/pallas_call | solution.py:161
Async XLA Ops:
  257.2 3.8 %copy-start = (f32[6528,384]{1,0:T(8,128)S(1)}, f32[6528,384]{1,0:T(8,128)}, u32[]{:S(2)}) copy-start(f32[6528,384]{1,0:T(8,128)} %get-tuple-element.25) | copy-start | bytes 30081028
  261.0 3.8 %copy-start.1 = (f32[6528,384]{1,0:T(8,128)S(1)}, f32[6528,384]{1,0:T(8,128)}, u32[]{:S(2)}) copy-start(f32[6528,384]{1,0:T(8,128)} %get-tuple-element.26) | copy-start | bytes 30081028

commit v4 on v3

--- a/solution.py
+++ b/solution.py
@@ -53,20 +53,29 @@
 
 
 def fetches(srcs, dsts, sems):
-    return [pltpu.make_async_copy(src, dst, sems.at[i]) for i, (src, dst) in enumerate(zip(srcs, dsts))]
-
-
-def forward_rows(x_ref, y_ref, w1_ref, w2_ref, p_ref, u_ref):
+    pairs = [(srcs[i].at[k], dsts[i].at[k]) for k in range(2) for i in range(2)] + [(srcs[2], dsts[2])]
+    return [pltpu.make_async_copy(src, dst, sems.at[i]) for i, (src, dst) in enumerate(pairs)]
+
+
+def forward_rows(x_ref, y_ref, w1_ref, w2_ref, p_ref, u_ref, loads):
     m = x_ref.shape[0] // SUB_COUNT
 
     def step(i, _):
+        def need(n):
+            @pl.when(i == 0)
+            def _():
+                loads[n].wait()
+
         at = pl.ds(pl.multiple_of(i * m, m), m)
         h = x_ref[at, :]
         for k in range(2):
+            need(2 * k)
             for j in TILES:
                 cs = slice(j * COLS, (j + 1) * COLS)
                 u_ref[:, cs] = gelu(mm(h, w1_ref[k, :, cs])).astype(BF16)
+            need(2 * k + 1)
             h = (h.astype(F32) + mm(u_ref[...], w2_ref[k])).astype(BF16)
+        need(4)
         y_ref[at, :] = mm(h, p_ref[...]).astype(BF16)
         return 0
 
@@ -75,7 +84,7 @@
 
 WEIGHTS = [
     pltpu.VMEM((2, WIDTH, FFN), BF16), pltpu.VMEM((2, FFN, WIDTH), BF16), pltpu.VMEM((WIDTH, WIDTH), BF16),
-    pltpu.SemaphoreType.DMA((3,))]
+    pltpu.SemaphoreType.DMA((5,))]
 INNER, OUTER = pl.BlockSpec(memory_space=pltpu.VMEM), pl.BlockSpec(memory_space=pltpu.HBM)
 SCALAR = pl.BlockSpec(memory_space=pltpu.SMEM)
 
@@ -84,9 +93,7 @@
     loads = fetches((w1_ref, w2_ref, p_ref), (w1, w2, p), w_sems)
     for load in loads:
         load.start()
-    for load in loads:
-        load.wait()
-    forward_rows(x_ref, y_ref, w1, w2, p, u_ref)
+    forward_rows(x_ref, y_ref, w1, w2, p, u_ref, loads)
 
 
 def tower_forward(rows, w1, w2, p):
@@ -168,7 +175,7 @@
             pltpu.SemaphoreType.DMA((2 * BLOCKS,)),
             pltpu.SemaphoreType.DMA((2 * BLOCKS,)),
         ],
-        compiler_params=pltpu.CompilerParams(vmem_limit_bytes=24 << 20),
+        compiler_params=pltpu.CompilerParams(vmem_limit_bytes=VMEM_MAX),
         name="unpack",
     )(q_blocks, d_blocks)
 
@@ -361,9 +368,7 @@
     doc = Gather(functools.partial(hop, me, docs_own, docs, (0, 336, 672, 1024), d_sems))
     doc.begin()
     docs[pl.ds(pl.multiple_of(me * CHUNK, CHUNK), CHUNK), :] = docs_own[...]
-    for load in loads:
-        load.wait()
-    forward_rows(x_ref, q_ref, w1, w2, p_w, u_ref)
+    forward_rows(x_ref, q_ref, w1, w2, p_w, u_ref, loads)
     doc.pass_on(2, 0)
     m_ref[...] = jnp.full_like(m_ref, LOW)
     lane = lax.broadcasted_iota(jnp.int32, (ROWS, 128), 1)
@@ -562,7 +567,6 @@
     places = mine, partner, peers = sum_places(me)
     greet(peers)
     queries = pltpu.make_async_copy(q_ref, q_buf, q_sem)
-    queries.start()
 
     def load(p, r):
         k = 8 * p + r
@@ -573,8 +577,10 @@
     sum_d = DeviceSum(places, lambda p, r: grads.at[mine[8 * p + r]], lambda p, r: grads.at[partner[8 * p + r]], out_d,
                       rest[4:8], rest[25:42])
     sum_q.start()
+    queries.start()
     for load in loads:
         load.start()
+    sum_q.swapped(FAR)
 
     def rows_of(k):
         return pl.ds(pl.multiple_of(lax.rem(me + k, ND) * ROWS, ROWS), ROWS)
@@ -589,7 +595,6 @@
     row = lax.broadcasted_iota(jnp.int32, (CHUNK, ROWS), 0)
     col = lax.broadcasted_iota(jnp.int32, (CHUNK, ROWS), 1)
     up_ref[...] = mm((probs(0) - jnp.where(row == col, scale, 0.0)).astype(BF16), q_buf[rows_of(0), :])
-    sum_q.swapped(FAR)
 
     def columns(i, _):
         @pl.when(i == 1)

time: 278 us -> 276 us (level)
  local copies, waits for them, and re-layouts: 7.69 us -> 0 us
  Pallas kernels: 265 us -> 271 us
    unnamed x4 -> x0, local copies, waits for them, and re-layouts: 7.69 us -> none
where the time goes in v4:
time: 276 us
  Pallas kernels  271 us (98%)
  between operations  3.1 us (1%)
    pallas_call x1, Pallas kernels, tail(): pl.pallas_call(tail_kernel, out_shape=[PACKED, PACKED], in_specs=[SCALAR]...  144 us
    pallas_call x1, Pallas kernels, gather_rows(): pl.pallas_call(gather_kernel, out_shape=[mine, jax.ShapeDtypeStruct((ND,...  68.1 us
    pallas_call x1, Pallas kernels, query_backward(): pl.pallas_call(query_kernel, out_shape=[PACKED, jax.ShapeDtypeStruct((BAT...  30.4 us
    pallas_call x1, Pallas kernels, tower_forward(): pl.pallas_call(forward_kernel, out_shape=jax.ShapeDtypeStruct(rows.shape,...  15 us
    pallas_call x1, Pallas kernels, unpack(): pl.pallas_call(unpack_kernel, out_shape=[jax.ShapeDtypeStruct(a, F32) for...  14.1 us

profile of v4, /device:TPU:0, one launch (start us, length us, event | category | flops | bytes accessed | tf_op | source)
XLA Modules:
  0.0 276.0 jit_solution(5242710216161227657)
XLA Ops:
  1.3 15.0 %tower_forward.1.docs_own.own_ref = bf16[1024,384]{1,0:T(8,128)(2,1)} custom-call(bf16[1024,384]{1,0:T(8,128)(2,1)} %bitcast.8, bf16[2,384,1536]{2,1,0:T(8,128)(2,1)} %w1_ref.7, bf16[2,1536,384]{2,1,0:T(8,128)(2,1)} %w2_ref.7, bf16[384,384]{1,0:T(8,128)(2,1)} %p_ref.7), custom_call_target="tpu_custom_call" | custom-call | tf_op jit(solution)/shard_map/tower_forward/pallas_call | solution.py:100
  16.3 68.1 %gather_rows.1 = (bf16[512,384]{1,0:T(8,128)(2,1)}, f32[16,8,512]{2,1,0:T(8,128)}, bf16[512,384]{1,0:T(8,128)(2,1)}) custom-call(f32[1]{0:T(128)} %bitcast.4.tau_ref, bf16[1024,384]{1,0:T(8,128)(2,1)} %tower_forward.1.docs_own.own_ref, bf16[512,384]{1,0:T(8,128)(2,1)} %x_ref.3, bf16[2,384,1536]{2,1,0:T(8,128)(2,1)} %w1_ref.6, bf16[2,1536,384]{2,1,0:T(8,128)(2,1)} %w2_ref.6, ...), custom_call_target="tpu_custom_call" | custom-call | tf_op jit(solution)/shard_map/gather_rows/pallas_call | solution.py:471
  84.4 1.6 slice_reduce_fusion
  86.7 30.4 %query_backward.1 = (f32[6528,384]{1,0:T(8,128)}, bf16[8192,384]{1,0:T(8,128)(2,1)}) custom-call(bf16[512,384]{1,0:T(8,128)(2,1)} %get-tuple-element.21.q_ref, bf16[512,384]{1,0:T(8,128)(2,1)} %x_ref.3, bf16[512,384]{1,0:T(8,128)(2,1)} %get-tuple-element.22.up_ref, bf16[2,384,1536]{2,1,0:T(8,128)(2,1)} %w1_ref.6, bf16[2,1536,384]{2,1,0:T(8,128)(2,1)} %w2_ref.6, ...), custom_call_target="tpu_custom_call" | custom-call | tf_op jit(solution)/shard_map/query_backward/pallas_call | solution.py:549
  117.1 143.6 %tail.1 = (f32[6528,384]{1,0:T(8,128)}, f32[6528,384]{1,0:T(8,128)}) custom-call(f32[1]{0:T(128)} %bitcast.5.tau_ref, f32[16,8,512]{2,1,0:T(8,128)} %get-tuple-element.20.stat_ref, bf16[1024,384]{1,0:T(8,128)(2,1)} %tower_forward.1.docs_own.own_ref, bf16[1024,384]{1,0:T(8,128)(2,1)} %bitcast.9, bf16[2,384,1536]{2,1,0:T(8,128)(2,1)} %w1_ref.7, ...), custom_call_target="tpu_custom_call" | custom-call | tf_op jit(solution)/shard_map/tail/pallas_call | solution.py:665
  260.7 14.1 %unpack.1 = (f32[2,384,1536]{2,1,0:T(8,128)}, f32[2,1536,384]{2,1,0:T(8,128)}, f32[384,384]{1,0:T(8,128)}, f32[2,384,1536]{2,1,0:T(8,128)}, f32[2,1536,384]{2,1,0:T(8,128)}, /*index=5*/f32[384,384]{1,0:T(8,128)}) custom-call(f32[17,384,384]{2,1,0:T(8,128)} %bitcast.6, f32[17,384,384]{2,1,0:T(8,128)} %bitcast.7), custom_call_target="tpu_custom_call" | custom-call | tf_op jit(solution)/shard_map/unpack/pallas_call | solution.py:168

commit v5 on v4

--- a/solution.py
+++ b/solution.py
@@ -59,23 +59,17 @@
 
 def forward_rows(x_ref, y_ref, w1_ref, w2_ref, p_ref, u_ref, loads):
     m = x_ref.shape[0] // SUB_COUNT
+    for load in loads:
+        load.wait()
 
     def step(i, _):
-        def need(n):
-            @pl.when(i == 0)
-            def _():
-                loads[n].wait()
-
         at = pl.ds(pl.multiple_of(i * m, m), m)
         h = x_ref[at, :]
         for k in range(2):
-            need(2 * k)
             for j in TILES:
                 cs = slice(j * COLS, (j + 1) * COLS)
                 u_ref[:, cs] = gelu(mm(h, w1_ref[k, :, cs])).astype(BF16)
-            need(2 * k + 1)
             h = (h.astype(F32) + mm(u_ref[...], w2_ref[k])).astype(BF16)
-        need(4)
         y_ref[at, :] = mm(h, p_ref[...]).astype(BF16)
         return 0
 
@@ -597,15 +591,15 @@
     up_ref[...] = mm((probs(0) - jnp.where(row == col, scale, 0.0)).astype(BF16), q_buf[rows_of(0), :])
 
     def columns(i, _):
+        @pl.when(i == 0)
+        def _():
+            sum_q.swapped(NEAR)
+
         @pl.when(i == 1)
         def _():
-            sum_q.swapped(NEAR)
+            sum_q.second(3)
 
         @pl.when(i == 2)
-        def _():
-            sum_q.second(3)
-
-        @pl.when(i == 3)
         def _():
             sum_q.second(2)
 
@@ -624,36 +618,39 @@
         grads[block * WIDTH:(block + 1) * WIDTH, :] += value
 
     def backward(i, _):
-        @pl.when(i == 2)
-        def _():
-            sum_q.finish()
-
-        @pl.when(i == 3)
-        def _():
-            sum_q.gather.pass_on(2, 0)
-
         def middle():
             @pl.when(i == 0)
             def _():
                 sum_q.third()
 
+        @pl.when(i == 1)
+        def _():
+            sum_q.finish()
+
+        @pl.when(i == 2)
+        def _():
+            sum_q.gather.pass_on(2, 0)
+
+        @pl.when(i == 3)
+        def _():
+            sum_q.gather.pass_on(1, 0)
+
         at = pl.ds(pl.multiple_of(i * m, m), m)
         backward_rows(x_ref[at, :], up_ref[at, :].astype(BF16), w1, w2, p_w, add, u_ref, s_ref, h_ref, dl_ref, middle)
         return 0
 
     lax.fori_loop(0, SUB_COUNT, backward, 0)
     sum_d.start()
-    sum_q.gather.pass_on(1, 0)
     sum_d.swapped(FAR)
-    sum_q.gather.pass_on(1, 1)
+    sum_q.gather.pass_on(0, 0, 1)
     sum_d.swapped(NEAR)
-    sum_q.gather.pass_on(0, 0, 1)
     sum_d.second(3)
     sum_q.gather.pass_on(0, 2)
     sum_d.second(2)
+    sum_d.third()
+    sum_q.gather.pass_on(1, 1)
+    sum_d.finish()
     sum_q.gather.pass_on(0, 3)
-    sum_d.third()
-    sum_d.finish()
     sum_d.gather.pass_on(2, 0)
     sum_d.gather.pass_on(1, 0, 1)
     sum_d.gather.pass_on(0, *range(4))

time: 276 us -> 270 us (0.978)
  Pallas kernels: 271 us -> 265 us
    pallas_call x1, Pallas kernels: 144 us -> 139 us  [tail(): pl.pallas_call(tail_kernel, out_shape=[PACKED, PACKED], in_specs=[SCALAR]...]
where the time goes in v5:
time: 270 us
  Pallas kernels  265 us (98%)
  between operations  3.1 us (1%)
    pallas_call x1, Pallas kernels, tail(): pl.pallas_call(tail_kernel, out_shape=[PACKED, PACKED], in_specs=[SCALAR]...  139 us
    pallas_call x1, Pallas kernels, gather_rows(): pl.pallas_call(gather_kernel, out_shape=[mine, jax.ShapeDtypeStruct((ND,...  68.1 us
    pallas_call x1, Pallas kernels, query_backward(): pl.pallas_call(query_kernel, out_shape=[PACKED, jax.ShapeDtypeStruct((BAT...  30.4 us
    pallas_call x1, Pallas kernels, unpack(): pl.pallas_call(unpack_kernel, out_shape=[jax.ShapeDtypeStruct(a, F32) for...  14.1 us
    pallas_call x1, Pallas kernels, tower_forward(): pl.pallas_call(forward_kernel, out_shape=jax.ShapeDtypeStruct(rows.shape,...  13.1 us

profile of v5, /device:TPU:0, one launch (start us, length us, event | category | flops | bytes accessed | tf_op | source)
XLA Modules:
  0.0 269.9 jit_solution(4346229992756870672)
XLA Ops:
  1.3 13.1 %tower_forward.1.docs_own.own_ref = bf16[1024,384]{1,0:T(8,128)(2,1)} custom-call(bf16[1024,384]{1,0:T(8,128)(2,1)} %bitcast.8, bf16[2,384,1536]{2,1,0:T(8,128)(2,1)} %w1_ref.7, bf16[2,1536,384]{2,1,0:T(8,128)(2,1)} %w2_ref.7, bf16[384,384]{1,0:T(8,128)(2,1)} %p_ref.7), custom_call_target="tpu_custom_call" | custom-call | tf_op jit(solution)/shard_map/tower_forward/pallas_call | solution.py:94
  14.4 68.1 %gather_rows.1 = (bf16[512,384]{1,0:T(8,128)(2,1)}, f32[16,8,512]{2,1,0:T(8,128)}, bf16[512,384]{1,0:T(8,128)(2,1)}) custom-call(f32[1]{0:T(128)} %bitcast.4.tau_ref, bf16[1024,384]{1,0:T(8,128)(2,1)} %tower_forward.1.docs_own.own_ref, bf16[512,384]{1,0:T(8,128)(2,1)} %x_ref.3, bf16[2,384,1536]{2,1,0:T(8,128)(2,1)} %w1_ref.6, bf16[2,1536,384]{2,1,0:T(8,128)(2,1)} %w2_ref.6, ...), custom_call_target="tpu_custom_call" | custom-call | tf_op jit(solution)/shard_map/gather_rows/pallas_call | solution.py:465
  82.6 1.6 slice_reduce_fusion
  84.8 30.4 %query_backward.1 = (f32[6528,384]{1,0:T(8,128)}, bf16[8192,384]{1,0:T(8,128)(2,1)}) custom-call(bf16[512,384]{1,0:T(8,128)(2,1)} %get-tuple-element.21.q_ref, bf16[512,384]{1,0:T(8,128)(2,1)} %x_ref.3, bf16[512,384]{1,0:T(8,128)(2,1)} %get-tuple-element.22.up_ref, bf16[2,384,1536]{2,1,0:T(8,128)(2,1)} %w1_ref.6, bf16[2,1536,384]{2,1,0:T(8,128)(2,1)} %w2_ref.6, ...), custom_call_target="tpu_custom_call" | custom-call | tf_op jit(solution)/shard_map/query_backward/pallas_call | solution.py:543
  115.3 139.4 %tail.1 = (f32[6528,384]{1,0:T(8,128)}, f32[6528,384]{1,0:T(8,128)}) custom-call(f32[1]{0:T(128)} %bitcast.5.tau_ref, f32[16,8,512]{2,1,0:T(8,128)} %get-tuple-element.20.stat_ref, bf16[1024,384]{1,0:T(8,128)(2,1)} %tower_forward.1.docs_own.own_ref, bf16[1024,384]{1,0:T(8,128)(2,1)} %bitcast.9, bf16[2,384,1536]{2,1,0:T(8,128)(2,1)} %w1_ref.7, ...), custom_call_target="tpu_custom_call" | custom-call | tf_op jit(solution)/shard_map/tail/pallas_call | solution.py:662
  254.7 14.1 %unpack.1 = (f32[2,384,1536]{2,1,0:T(8,128)}, f32[2,1536,384]{2,1,0:T(8,128)}, f32[384,384]{1,0:T(8,128)}, f32[2,384,1536]{2,1,0:T(8,128)}, f32[2,1536,384]{2,1,0:T(8,128)}, /*index=5*/f32[384,384]{1,0:T(8,128)}) custom-call(f32[17,384,384]{2,1,0:T(8,128)} %bitcast.6, f32[17,384,384]{2,1,0:T(8,128)} %bitcast.7), custom_call_target="tpu_custom_call" | custom-call | tf_op jit(solution)/shard_map/unpack/pallas_call | solution.py:162
